TPU v7x, 256 devices: a whole 4x4x8 slice. The times are simulated.
256 devices in a mesh: rows: 64 (over z, y, core), mem: 4 (over x).
Axes of the slice: x: 4, y: 4, z: 8, core: 2. Of those that a mesh axis runs over, the one named last changes fastest.
Arguments:
- control: bfloat16 [16, 32, 2, 512, 512], P('mem', None, None, 'rows'), may hold values from -6 to 6
- vert_root: float32 [32, 32], replicated, may hold values from -1 to 1
- loc_spec: float32 [512], replicated, may hold values from 0.1 to 1
- legendre: bfloat16 [512, 512, 768], P('rows'), as said below
- wave_table: int32 [512], replicated, may hold values from 0 to 511, as said below
- lat_order: int32 [768], replicated, may hold values from 0 to 767, each once
- perturb: bfloat16 [768, 16, 32, 1536], P('rows', None, 'mem'), may hold values from -3 to 3
Outputs:
- increment: bfloat16 [768, 32, 1536], P('rows', 'mem')
Inputs may be any that keep to these rules, and one draw needn't show every extreme that they name: `wave_table`: every zonal wavenumber 0 to 511 sits in exactly one slot; the slots held by one index of rows are pairs m and 511 - m. legendre[s, n, t] is zero where n < wave_table[s]. `lat_order`: a permutation.
All inputs are finite; a program needn't handle non-finite values.
Results may differ from a plain program's by a relative error of at most 0.0085.
Values may be sent and summed in bfloat16 or wider, within the bound.
No kernel may reach another device: no remote copies, remote signals or barrier semaphores. Data moves between devices by JAX's collectives and lax.ppermute only.
A program may use at most 128 MiB of HBM per device.

v0:
```python
import math

import jax
import jax.numpy as jnp
from jax import lax
from jax.sharding import PartitionSpec as P


def make_basis(wave_table, lon_count):
    longitude = lax.iota(jnp.int32, lon_count)
    phases = wave_table[:, None] * longitude[None, :] % lon_count
    angles = phases.astype(jnp.float32) * (2.0 * math.pi / lon_count)
    weights = jnp.where(wave_table == 0, 1.0, 2.0).astype(jnp.float32)[:, None]
    return jnp.stack([weights * jnp.cos(angles), -weights * jnp.sin(angles)]).astype(jnp.bfloat16)


def synthesize(level_block, legendre, lat_order, zonal_basis):
    fourier = jnp.einsum(
        "snt,klrsn->strkl", legendre, level_block, preferred_element_type=jnp.float32
    )
    fourier = jnp.take(fourier, lat_order, axis=1)
    four_shape = fourier.shape
    fourier = fourier.reshape(four_shape[0], four_shape[1], -1).astype(jnp.bfloat16)
    fourier = lax.all_to_all(fourier, "rows", split_axis=1, concat_axis=0, tiled=True)
    fourier = fourier.reshape(
        fourier.shape[0], fourier.shape[1], four_shape[2], four_shape[3], four_shape[4]
    )
    fields = jnp.einsum("sjrkl,rsx->jklx", fourier, zonal_basis, preferred_element_type=jnp.float32)
    return fields.astype(jnp.bfloat16)


def member_sum(fields, member_ptb):
    return jnp.sum(fields.astype(jnp.float32) * member_ptb.astype(jnp.float32), axis=1)


def shards(control, vert_root, loc_spec, legendre, wave_table, lat_order, perturb):
    mem_count = lax.axis_size("mem")
    members_dev, levels, _, slot_count, wave_count = control.shape
    level_share = levels // mem_count
    batch_count = 1
    level_batch = level_share // batch_count
    scaled = control.astype(jnp.float32) * loc_spec
    spectra = jnp.einsum(
        "lv,kvrsn->klrsn", vert_root, scaled, precision=lax.Precision.HIGHEST
    ).astype(jnp.bfloat16)
    zonal_basis = make_basis(wave_table, perturb.shape[3])
    grouped = spectra.reshape(
        members_dev, mem_count, batch_count, level_batch, 2, slot_count, wave_count
    )
    level_block = grouped[:, :, 0].reshape(
        members_dev, mem_count * level_batch, 2, slot_count, wave_count
    )
    fields = synthesize(level_block, legendre, lat_order, zonal_basis)
    fields = lax.all_to_all(fields, "mem", split_axis=2, concat_axis=1, tiled=True)
    pieces = member_sum(fields, perturb)
    return pieces.astype(jnp.bfloat16)


def solution(mesh):
    return jax.shard_map(
        shards,
        mesh=mesh,
        in_specs=(
            P("mem", None, None, "rows", None),
            P(),
            P(),
            P("rows", None, None),
            P(),
            P(),
            P("rows", None, "mem", None),
        ),
        out_specs=P("rows", "mem", None),
        check_vma=False,
    )
```

profile of v0, /device:TPU:1, one launch (start us, length us, event | category | flops | bytes accessed | tf_op | source)
XLA Modules:
  0.0 268.7 jit_solution(8176446546091429592)
XLA Ops:
  0.0 0.0 copy-start
  0.0 0.7 compare_select_fusion
  0.7 0.7 compare_and_fusion
  1.4 0.0 slice-start
  1.4 2.4 convert_multiply_fusion
  3.8 0.0 copy-done
  3.8 0.0 slice-start.1
  3.8 7.2 %fusion.7 = bf16[4,2,8,512,32]{3,4,1,0,2:T(8,128)(2,1)S(1)} fusion(f32[4,32,2,8,512]{4,3,2,1,0:T(8,128)S(1)} %convert_multiply_fusion, f32[32,32]{1,0:T(8,128)S(1)} %copy-done), kind=kOutput, calls=%fused_computation.11 | convolution fusion | flops 402653184 | bytes 6295552 | tf_op jit(solution)/shard_map/lv,kvrsn->klrsn/dot_general | solution.py:43
  11.0 0.0 slice-done
  11.0 0.0 slice-done.1
  11.0 1.8 fusion.16
  12.9 17.4 %copy.16 = bf16[8,768,2,4,32]{4,0,3,2,1:T(8,128)(2,1)} copy(bf16[8,768,2,4,32]{1,4,2,3,0:T(8,128)(2,1)S(1)} %fusion.16) | data formatting | bytes 6291456 | tf_op jit(solution)/shard_map/snt,klrsn->strkl/transpose | solution.py:18
  30.3 24.4 %gather_fusion = bf16[768,8,2,4,32]{4,1,3,2,0:T(8,128)(2,1)} fusion(bf16[8,768,2,4,32]{4,0,3,2,1:T(8,128)(2,1)} %copy.16, s32[1024]{0:T(1024)S(1)} %pad_clamp_fusion), kind=kCustom, calls=%fused_computation | custom fusion | bytes 6294528 | tf_op jit(solution)/shard_map/jit(_take)/gather | solution.py:21
  54.7 14.6 %copy.17 = bf16[8,768,2,4,32]{1,4,3,2,0:T(8,128)(2,1)} copy(bf16[8,768,2,4,32]{4,0,3,2,1:T(8,128)(2,1)} %bitcast.42) | data formatting | bytes 6291456 | tf_op jit(solution)/shard_map/jit(_take)/gather | solution.py:21
  69.2 2.4 fusion.4
  71.7 3.5 %copy.18 = bf16[8,768,256]{2,0,1:T(8,128)(2,1)} copy(bf16[8,768,256]{1,2,0:T(8,128)(2,1)S(1)} %fusion.4) | data formatting | bytes 6291456 | tf_op jit(solution)/shard_map/convert_element_type | solution.py:23
  75.1 0.0 copy-start.4
  75.1 13.3 %all-to-all-start = ((bf16[8,768,256]{2,0,1:T(8,128)(2,1)}), bf16[8,768,256]{2,0,1:T(8,128)(2,1)S(1)}, u32[]{:S(2)}, u32[]{:S(2)}) async-start(bf16[8,768,256]{2,0,1:T(8,128)(2,1)} %copy.18), calls=%async_computation | async-start | bytes 6291456 | tf_op jit(solution)/shard_map/all_to_all | solution.py:24
  88.4 0.0 copy-done.4
  88.4 15.3 %multiply_convert_fusion.1 = (bf16[1,512,1536]{2,1,0:T(8,128)(2,1)}, bf16[1,512,1536]{2,1,0:T(8,128)(2,1)}) fusion(s32[512]{0:T(512)S(1)} %copy-done.4, f32[512]{0:T(512)S(1)} %get-tuple-element.7, f32[512]{0:T(512)S(1)} %get-tuple-element.8), kind=kLoop, calls=%fused_computation.20 | loop fusion | flops 10223616 | bytes 3151872 | tf_op jit(solution)/shard_map/convert.3
  103.7 57.1 %all-to-all-done = bf16[8,768,256]{2,0,1:T(8,128)(2,1)S(1)} async-done(((bf16[8,768,256]{2,0,1:T(8,128)(2,1)}), bf16[8,768,256]{2,0,1:T(8,128)(2,1)S(1)}, u32[]{:S(2)}, u32[]{:S(2)}) %all-to-all-start) | async-done | bytes 3145760 | tf_op jit(solution)/shard_map/all_to_all | solution.py:24
  160.8 1.9 copy.19
  162.7 0.0 copy-start.2
  162.7 0.0 copy-start.3
  162.7 17.2 %reshape.137 = bf16[512,12,2,4,32]{4,3,2,0,1:T(4,128)(2,1)} reshape(bf16[64,8,12,256]{3,1,0,2:T(8,128)(2,1)} %copy.19) | data formatting | bytes 6291456 | tf_op jit(solution)/shard_map/reshape | solution.py:25
  179.9 0.0 copy-done.2
  179.9 0.0 copy-done.3
  179.9 8.9 %bitcast_convert_fusion = bf16[12,4,32,1536]{3,2,1,0:T(8,128)(2,1)S(1)} fusion(bf16[512,12,2,4,32]{4,3,2,0,1:T(4,128)(2,1)} %reshape.137, bf16[1,512,1536]{2,1,0:T(8,128)(2,1)S(1)} %copy-done.3, bf16[1,512,1536]{2,1,0:T(8,128)(2,1)S(1)} %copy-done.2), kind=kOutput, calls=%fused_computation.4 | convolution fusion | flops 4835770368 | bytes 11010048 | tf_op jit(solution)/shard_map/sjrkl,rsx->jklx/dot_general | solution.py:28
  188.9 3.6 %copy.21 = bf16[12,4,32,1536]{3,1,0,2:T(4,128)(2,1)S(1)} copy(bf16[12,4,32,1536]{3,2,1,0:T(8,128)(2,1)S(1)} %bitcast_convert_fusion) | data formatting | bytes 9437184 | tf_op jit(solution)/shard_map/convert_element_type | solution.py:29
  192.5 56.0 %all_to_all.24 = bf16[12,4,32,1536]{3,1,0,2:T(4,128)(2,1)} all-to-all(bf16[12,4,32,1536]{3,1,0,2:T(4,128)(2,1)S(1)} %copy.21), channel_id=1, replica_groups=mesh['rows'=64,'mem'=4] {'mem'}, dimensions={2} | all-to-all | bytes 9437184 | tf_op jit(solution)/shard_map/all_to_all | solution.py:54
  248.5 3.8 %convert_bitcast_fusion = f32[12,4,4,8,1536]{4,2,0,3,1:T(4,128)S(1)} fusion(bf16[12,4,4,8,1536]{4,1,0,3,2:T(4,128)(2,1)} %bitcast.44), kind=kLoop, calls=%fused_computation.3 | loop fusion | flops 2359296 | bytes 14155776 | tf_op jit(solution)/shard_map/convert_element_type | solution.py:33
  252.3 9.1 %copy.22 = f32[12,4,4,8,1536]{4,3,2,1,0:T(8,128)} copy(f32[12,4,4,8,1536]{4,2,0,3,1:T(4,128)S(1)} %convert_bitcast_fusion) | data formatting | bytes 18874368 | tf_op jit(solution)/shard_map/convert_element_type | solution.py:33
  261.4 0.0 copy-start.1
  261.4 7.3 %multiply_reduce_fusion = bf16[12,8,1536]{2,1,0:T(8,128)(2,1)} fusion(f32[12,16,8,1536]{3,2,1,0:T(8,128)} %bitcast.43, bf16[12,16,8,1536]{3,2,1,0:T(8,128)(2,1)} %param.13), kind=kLoop, calls=%fused_computation.5 | loop fusion | flops 6930432 | bytes 14450688 | tf_op jit(solution)/shard_map/reduce_sum | solution.py:33
  268.7 0.0 copy-done.1
  (3 shorter events, 0.0 us)
Async XLA Ops:
  0.0 3.8 %copy-start = (f32[32,32]{1,0:T(8,128)S(1)}, f32[32,32]{1,0:T(8,128)}, u32[]{:S(2)}) copy-start(f32[32,32]{1,0:T(8,128)} %param.8) | copy-start | bytes 12292
  1.4 9.6 %slice-start = ((s8[6291456]{0:T(1024)(128)(4,1)}), s8[4194304]{0:T(1024)(128)(4,1)S(1)}, s32[]{:S(2)}) async-start(s8[6291456]{0:T(1024)(128)(4,1)} %bitcast.46), calls=%async_computation.2 | async-start | bytes 8388608
  3.8 7.2 %slice-start.1 = ((s8[6291456]{0:T(1024)(128)(4,1)}), s8[2097152]{0:T(1024)(128)(4,1)S(1)}, s32[]{:S(2)}) async-start(s8[6291456]{0:T(1024)(128)(4,1)} %bitcast.46), calls=%async_computation.3 | async-start | bytes 4194304
  75.1 13.3 %copy-start.4 = (s32[512]{0:T(512)S(1)}, s32[512]{0:T(512)}, u32[]{:S(2)}) copy-start(s32[512]{0:T(512)} %param.11) | copy-start | bytes 6148
  75.1 85.7 %all-to-all-start = ((bf16[8,768,256]{2,0,1:T(8,128)(2,1)}), bf16[8,768,256]{2,0,1:T(8,128)(2,1)S(1)}, u32[]{:S(2)}, u32[]{:S(2)}) async-start(bf16[8,768,256]{2,0,1:T(8,128)(2,1)} %copy.18), calls=%async_computation | async-start | bytes 6291456 | tf_op jit(solution)/shard_map/all_to_all | solution.py:24
  162.7 17.2 %copy-start.2 = (bf16[1,512,1536]{2,1,0:T(8,128)(2,1)S(1)}, bf16[1,512,1536]{2,1,0:T(8,128)(2,1)}, u32[]{:S(2)}) copy-start(bf16[1,512,1536]{2,1,0:T(8,128)(2,1)} %get-tuple-element.5) | copy-start | bytes 4718596
  162.7 17.2 %copy-start.3 = (bf16[1,512,1536]{2,1,0:T(8,128)(2,1)S(1)}, bf16[1,512,1536]{2,1,0:T(8,128)(2,1)}, u32[]{:S(2)}) copy-start(bf16[1,512,1536]{2,1,0:T(8,128)(2,1)} %get-tuple-element.6) | copy-start | bytes 4718596
  261.4 7.3 %copy-start.1 = (f32[32,32]{1,0:T(8,128)S(1)}, f32[32,32]{1,0:T(8,128)}, u32[]{:S(2)}) copy-start(f32[32,32]{1,0:T(8,128)} %param.8) | copy-start | bytes 12292
where the time goes:
time: 271 us; the launch traced here: 269 us
  local copies, waits for them, and re-layouts  91.7 us (34%)
  waiting for transfers between devices  57.1 us (21%)
  blocking collectives  56 us (21%)
  other arithmetic  32.6 us (12%)
  matrix products  17.9 us (7%)
  starting transfers between devices  13.3 us (5%)
    all_to_all x1, waiting for transfers between devices, synthesize(): lax.all_to_all(fourier, 'rows', split_axis=1, concat_axis=0, tiled=True)  57.1 us
    all_to_all x1, blocking collectives, shards(): lax.all_to_all(fields, 'mem', split_axis=2, concat_axis=1, tiled=True)  56 us
    gather x2, local copies, waits for them, and re-layouts, synthesize(): fourier = jnp.take(fourier, lat_order, axis=1)  39 us
    transpose x1, local copies, waits for them, and re-layouts, synthesize(): jnp.einsum('snt,klrsn->strkl', legendre, level_block, preferred_element_t...  17.4 us
    reshape x1, local copies, waits for them, and re-layouts, synthesize(): fourier.reshape(fourier.shape[0], fourier.shape[1], four_shape[2], four_s...  17.2 us
    another operation x1, other arithmetic  15.3 us
    all_to_all x1, starting transfers between devices, synthesize(): lax.all_to_all(fourier, 'rows', split_axis=1, concat_axis=0, tiled=True)  13.3 us
    convert_element_type x1, local copies, waits for them, and re-layouts, member_sum(): fields.astype(jnp.float32) * member_ptb.astype(jnp.float32)  9.1 us
  transfers between devices with their start and end apart: 1, of which 1 were waited for; matrix products, arithmetic and copies ran while one was open for 6% of the time, Pallas kernels for 0%

commit v1 on v0

v1 whole, which is shorter than its diff:
```python
import math

import jax
import jax.numpy as jnp
from jax import lax
from jax.experimental import pallas as pl
from jax.experimental.pallas import tpu as pltpu
from jax.sharding import PartitionSpec as P

F32 = jnp.float32
BF16 = jnp.bfloat16
SUB = 4
PITCH = 200


def dot(a, b, dims):
    return lax.dot_general(a, b, (dims, ((), ())), preferred_element_type=F32)


def front_kernel(root_ref, loc_ref, lat_ref, ctrl_ref, leg_ref, out_ref, spec_scr, perm_scr, stage_scr):
    slot = pl.program_id(0)
    slots = pl.num_programs(0)
    members = ctrl_ref.shape[0]
    lats = perm_scr.shape[0]
    groups = lats // SUB

    @pl.when(slot == 0)
    def _():
        lat_col = jnp.transpose(jnp.broadcast_to(lat_ref[...].astype(F32), (8, lats)))[:, :1]
        cols = lax.broadcasted_iota(jnp.int32, (lats, lats), 1).astype(F32)
        perm_scr[...] = jnp.where(cols == lat_col, 1.0, 0.0).astype(BF16)
        root = root_ref[...]
        high = root.astype(BF16)
        low = (root - high.astype(F32)).astype(BF16)
        rows = lax.broadcasted_iota(jnp.int32, (512, 32), 0)
        lanes = lax.broadcasted_iota(jnp.int32, (512, 32), 1)
        pick_l = jnp.where(rows % 32 == lanes, 1.0, 0.0).astype(BF16)
        rows = lax.broadcasted_iota(jnp.int32, (32, 512), 0)
        lanes = lax.broadcasted_iota(jnp.int32, (32, 512), 1)
        pick_v = jnp.where(rows == lanes // 16, 1.0, 0.0).astype(BF16)
        rows = lax.broadcasted_iota(jnp.int32, (512, 512), 0)
        lanes = lax.broadcasted_iota(jnp.int32, (512, 512), 1)
        same = rows // 32 == lanes % 16
        mixes = []
        for part in (high, low):
            spread = dot(pick_l, part, ((1,), (0,))).astype(BF16)
            spread = dot(spread, pick_v, ((1,), (0,)))
            mixes.append(jnp.where(same, spread, 0.0).astype(BF16))
        for k in range(members):
            coefs = ctrl_ref[k].reshape(512, 512)
            mixed = dot(mixes[0], coefs, ((1,), (0,))) + dot(mixes[1], coefs, ((1,), (0,)))
            mixed = mixed * loc_ref[...]
            for r in range(2):
                for s in range(8):
                    for q in range(4):
                        src = (r * 8 + s) * 32 + q * 8
                        spec_scr[s, pl.ds(q * 64 + r * 32 + k * 8, 8), :] = mixed[src:src + 8]

    spec = spec_scr[slot].astype(BF16)
    fourier = dot(spec, leg_ref[0], ((1,), (0,))).astype(BF16)
    sorted_rows = dot(perm_scr[...], fourier, ((1,), (1,)))
    lane_group = lax.broadcasted_iota(jnp.int32, (groups, 128), 1) // 32
    base = pl.multiple_of(slot * PITCH, 8)
    for half in range(2):
        parts = [sorted_rows[a * groups:(a + 1) * groups, half * 128:(half + 1) * 128] for a in range(SUB)]
        turned = []
        for d in range(SUB):
            mix = parts[d]
            for p in range(1, SUB):
                mix = jnp.where(lane_group == p, parts[(p + d) % SUB], mix)
            turned.append(pltpu.roll(mix, 32 * d, 1) if d else mix)
        for q in range(4):
            piece = turned[(0 - q) % SUB]
            for a in range(1, SUB):
                piece = jnp.where(lane_group == a, turned[(a - q) % SUB], piece)
            stage_scr[half * 4 + q, pl.ds(base, groups), :] = piece

    @pl.when(slot == slots - 1)
    def _():
        def emit(row, carry):
            for third in range(3):
                for q in range(4):
                    tiles = [stage_scr[q * 2 + r, pl.ds(row * 3 + third, 8, stride=PITCH), :] for r in range(2)]
                    out_ref[row, q, third] = jnp.concatenate(tiles, axis=0).astype(BF16)
            return carry
        lax.fori_loop(0, 64, emit, 0)


def front(control, vert_root, loc_spec, legendre, lat_order):
    members, levels, _, slots, waves = control.shape
    lats = legendre.shape[2]
    ctrl = control.reshape(members, levels, 2 * slots, waves)
    lat_row = lat_order.reshape(lats // SUB, SUB).T.reshape(1, lats)
    return pl.pallas_call(
        front_kernel,
        grid=(slots,),
        in_specs=[
            pl.BlockSpec((levels, levels), lambda s: (0, 0)),
            pl.BlockSpec((1, waves), lambda s: (0, 0)),
            pl.BlockSpec((1, lats), lambda s: (0, 0)),
            pl.BlockSpec(ctrl.shape, lambda s: (0, 0, 0, 0)),
            pl.BlockSpec((1, waves, lats), lambda s: (s, 0, 0)),
        ],
        out_specs=pl.BlockSpec((64, 4, 3, 16, 128), lambda s: (0, 0, 0, 0, 0)),
        out_shape=jax.ShapeDtypeStruct((64, 4, 3, 16, 128), BF16),
        scratch_shapes=[
            pltpu.VMEM((slots, 256, waves), F32),
            pltpu.VMEM((lats, lats), BF16),
            pltpu.VMEM((8, slots * PITCH, 128), F32),
        ],
        compiler_params=pltpu.CompilerParams(vmem_limit_bytes=60 * 1024 * 1024),
        name="front",
    )(vert_root, loc_spec.reshape(1, waves), lat_row, ctrl, legendre)


def make_basis(wave_table, lon_count):
    waves = wave_table.reshape(-1, 1, 8, 1)
    longitude = lax.iota(jnp.int32, lon_count)
    phases = waves * longitude % lon_count
    angles = phases.astype(F32) * (2.0 * math.pi / lon_count)
    weights = jnp.where(waves == 0, 1.0, 2.0).astype(F32)
    pair = jnp.concatenate([weights * jnp.cos(angles), -weights * jnp.sin(angles)], axis=1)
    return pair.astype(BF16).reshape(-1, lon_count)


COLS = 256


def back_kernel(recv_ref, basis_ref, ptb_ref, out_ref, turn_scr):
    for q in range(4):
        coefs = recv_ref[:, q, 0].reshape(1024, 128)
        turn_scr[pl.ds(q * 128, 128), :] = jnp.transpose(coefs)
    for c in range(basis_ref.shape[1] // COLS):
        cols = pl.ds(c * COLS, COLS)
        field = dot(turn_scr[...], basis_ref[:, cols], ((1,), (0,))).astype(BF16).astype(F32)
        field = field.reshape(4, SUB, 4, 8, COLS)
        for a in range(SUB):
            total = None
            for q in range(4):
                for k in range(4):
                    term = field[q, a, k] * ptb_ref[a, q * 4 + k, :, cols].astype(F32)
                    total = term if total is None else total + term
            out_ref[a, :, cols] = total.astype(BF16)


def back(recv, basis, perturb):
    lats, members, levels, lons = perturb.shape
    return pl.pallas_call(
        back_kernel,
        grid=(3,),
        in_specs=[
            pl.BlockSpec((64, 4, 1, 16, 128), lambda j: (0, 0, j, 0, 0)),
            pl.BlockSpec((1024, lons), lambda j: (0, 0)),
            pl.BlockSpec((SUB, members, levels, lons), lambda j: (j, 0, 0, 0)),
        ],
        out_specs=pl.BlockSpec((SUB, levels, lons), lambda j: (j, 0, 0)),
        out_shape=jax.ShapeDtypeStruct((lats, levels, lons), BF16),
        scratch_shapes=[pltpu.VMEM((512, 1024), BF16)],
        compiler_params=pltpu.CompilerParams(vmem_limit_bytes=60 * 1024 * 1024),
        name="back",
    )(recv, basis, perturb)


def shards(control, vert_root, loc_spec, legendre, wave_table, lat_order, perturb):
    send = front(control, vert_root, loc_spec, legendre, lat_order)
    recv = lax.all_to_all(send.reshape(256, 3, 16, 128), ("rows", "mem"), 0, 0, tiled=True)
    basis = make_basis(wave_table, perturb.shape[3])
    return back(recv.reshape(64, 4, 3, 16, 128), basis, perturb)


def solution(mesh):
    return jax.shard_map(
        shards,
        mesh=mesh,
        in_specs=(
            P("mem", None, None, "rows", None),
            P(),
            P(),
            P("rows", None, None),
            P(),
            P(),
            P("rows", None, "mem", None),
        ),
        out_specs=P("rows", "mem", None),
        check_vma=False,
    )
```

time: 271 us -> 121 us (0.45)
  local copies, waits for them, and re-layouts: 91.7 us -> 3.31 us
  blocking collectives: 56 us -> 0 us
  Pallas kernels: 0 us -> 25.8 us
  matrix products: 17.9 us -> 0 us
  other arithmetic: 32.6 us -> 15.7 us
  waiting for transfers between devices: 57.1 us -> 60.1 us
    all_to_all x1 -> x0, blocking collectives: 56 us -> none  [shards(): lax.all_to_all(fields, 'mem', split_axis=2, concat_axis=1, tiled=True)]
    gather x2 -> x0, local copies, waits for them, and re-layouts: 39 us -> none  [synthesize(): fourier = jnp.take(fourier, lat_order, axis=1)]
    pallas_call x0 -> x2, Pallas kernels: none -> 25.8 us  [the longest x1 16.8 us: front(): pl.pallas_call(front_kernel, grid=(slots,), in_specs=[pl.BlockSpec((level...]
    dot_general x3 -> x0, matrix products: 17.9 us -> none  [the longest x1 8.91 us: synthesize(): jnp.einsum('sjrkl,rsx->jklx', fourier, zonal_basis, preferred_element_typ...]
    transpose x1, local copies, waits for them, and re-layouts: 17.4 us -> 0.07 us  [front(): lat_row = lat_order.reshape(lats // SUB, SUB).T.reshape(1, lats)]
    convert_element_type x3 -> x0, local copies, waits for them, and re-layouts: 16.2 us -> none  [the longest x1 9.1 us: member_sum(): fields.astype(jnp.float32) * member_ptb.astype(jnp.float32)]
    reshape x1 -> x3, local copies, waits for them, and re-layouts: 17.2 us -> 1.56 us  [the longest x2 1.48 us: front(): lat_row = lat_order.reshape(lats // SUB, SUB).T.reshape(1, lats)]
    reduce_sum x1 -> x0, other arithmetic: 7.33 us -> none  [member_sum(): jnp.sum(fields.astype(jnp.float32) * member_ptb.astype(jnp.float32), axis=1)]
  transfers between devices with their start and end apart: 1 -> 1, of which waited for: 1 -> 1; matrix products, arithmetic and copies ran while one was open for 6% -> 13% of each run, Pallas kernels for 0% -> 0%
where the time goes in v1:
time: 121 us
  waiting for transfers between devices  60.1 us (50%)
  Pallas kernels  25.8 us (21%)
  other arithmetic  15.7 us (13%)
  starting transfers between devices  15.6 us (13%)
  local copies, waits for them, and re-layouts  3.31 us (3%)
    all_to_all x1, waiting for transfers between devices, shards(): lax.all_to_all(send.reshape(256, 3, 16, 128), ('rows', 'mem'), 0, 0, tile...  60.1 us
    pallas_call x1, Pallas kernels, front(): pl.pallas_call(front_kernel, grid=(slots,), in_specs=[pl.BlockSpec((level...  16.8 us
    all_to_all x1, starting transfers between devices, shards(): lax.all_to_all(send.reshape(256, 3, 16, 128), ('rows', 'mem'), 0, 0, tile...  15.6 us
    another operation x1, other arithmetic  13.8 us
    pallas_call x1, Pallas kernels, back(): pl.pallas_call(back_kernel, grid=(3,), in_specs=[pl.BlockSpec((64, 4, 1,...  9.06 us
  transfers between devices with their start and end apart: 1, of which 1 were waited for; matrix products, arithmetic and copies ran while one was open for 13% of the time, Pallas kernels for 0%

profile of v1, /device:TPU:1, one launch (start us, length us, event | category | flops | bytes accessed | tf_op | source)
XLA Modules:
  0.0 120.7 jit_solution(17050349250944816256)
XLA Ops:
  0.0 0.8 reshape.102
  0.8 0.1 copy.8
  0.9 0.7 reshape.103.lat_ref
  1.6 16.8 %front.1 = bf16[64,4,3,16,128]{4,3,2,1,0:T(8,128)(2,1)} custom-call(f32[32,32]{1,0:T(8,128)} %root_ref.1, f32[1,512]{1,0:T(1,128)} %bitcast.11, s32[1,768]{1,0:T(1,128)} %reshape.103.lat_ref, bf16[4,32,16,512]{3,2,1,0:T(8,128)(2,1)} %bitcast.9, bf16[8,512,768]{2,1,0:T(8,128)(2,1)} %leg_ref.1), custom_call_target="tpu_custom_call" | custom-call | tf_op jit(solution)/shard_map/front/pallas_call | solution.py:94
  18.3 0.0 copy-start.1
  18.3 15.6 %all-to-all-start = ((bf16[256,3,16,128]{3,2,1,0:T(8,128)(2,1)}), bf16[256,3,16,128]{3,2,1,0:T(8,128)(2,1)S(1)}, u32[]{:S(2)}, u32[]{:S(2)}) async-start(bf16[256,3,16,128]{3,2,1,0:T(8,128)(2,1)} %bitcast.7), calls=%async_computation | async-start | bytes 6291456 | tf_op jit(solution)/shard_map/all_to_all | solution.py:166
  34.0 0.0 copy-done.1
  34.0 0.1 reshape.107
  34.1 13.8 %multiply_convert_fusion.1 = (bf16[64,1,8,1536]{3,2,1,0:T(8,128)(2,1)S(1)}, bf16[64,1,8,1536]{3,2,1,0:T(8,128)(2,1)S(1)}) fusion(s32[64,8]{1,0:T(8,128)S(1)} %reshape.107, f32[64,8]{1,0:T(8,128)S(1)} %get-tuple-element.7, f32[64,8]{1,0:T(8,128)S(1)} %get-tuple-element.8), kind=kLoop, calls=%fused_computation.5 | loop fusion | flops 10223616 | bytes 3151872 | tf_op jit(solution)/shard_map/convert
  47.9 2.0 %pad_maximum_fusion = bf16[64,2,8,1536]{3,2,1,0:T(8,128)(2,1)} fusion(bf16[64,1,8,1536]{3,2,1,0:T(8,128)(2,1)S(1)} %get-tuple-element.6, bf16[64,1,8,1536]{3,2,1,0:T(8,128)(2,1)S(1)} %get-tuple-element.5), kind=kLoop, calls=%fused_computation.3 | loop fusion | flops 1572864 | bytes 6291456 | tf_op jit(solution)/shard_map/concatenate | solution.py:122
  49.9 60.1 %all-to-all-done = bf16[256,3,16,128]{3,2,1,0:T(8,128)(2,1)S(1)} async-done(((bf16[256,3,16,128]{3,2,1,0:T(8,128)(2,1)}), bf16[256,3,16,128]{3,2,1,0:T(8,128)(2,1)S(1)}, u32[]{:S(2)}, u32[]{:S(2)}) %all-to-all-start) | async-done | bytes 3145760 | tf_op jit(solution)/shard_map/all_to_all | solution.py:166
  109.9 0.0 copy-start
  109.9 1.7 %copy-done = bf16[256,3,16,128]{3,2,1,0:T(8,128)(2,1)} copy-done((bf16[256,3,16,128]{3,2,1,0:T(8,128)(2,1)}, bf16[256,3,16,128]{3,2,1,0:T(8,128)(2,1)S(1)}, u32[]{:S(2)}) %copy-start) | copy-done | bytes 3145752
  111.6 9.1 %back.1 = bf16[12,8,1536]{2,1,0:T(8,128)(2,1)} custom-call(bf16[64,4,3,16,128]{4,3,2,1,0:T(8,128)(2,1)} %bitcast.6, bf16[1024,1536]{1,0:T(8,128)(2,1)} %bitcast.8, bf16[12,16,8,1536]{3,2,1,0:T(8,128)(2,1)} %ptb_ref.1), custom_call_target="tpu_custom_call" | custom-call | tf_op jit(solution)/shard_map/back/pallas_call | solution.py:148
  (1 shorter events, 0.0 us)
Async XLA Ops:
  18.3 15.7 %copy-start.1 = (s32[512]{0:T(512)S(1)}, s32[512]{0:T(512)}, u32[]{:S(2)}) copy-start(s32[512]{0:T(512)} %param.11) | copy-start | bytes 6148
  18.3 91.6 %all-to-all-start = ((bf16[256,3,16,128]{3,2,1,0:T(8,128)(2,1)}), bf16[256,3,16,128]{3,2,1,0:T(8,128)(2,1)S(1)}, u32[]{:S(2)}, u32[]{:S(2)}) async-start(bf16[256,3,16,128]{3,2,1,0:T(8,128)(2,1)} %bitcast.7), calls=%async_computation | async-start | bytes 6291456 | tf_op jit(solution)/shard_map/all_to_all | solution.py:166
  109.9 1.7 %copy-start = (bf16[256,3,16,128]{3,2,1,0:T(8,128)(2,1)}, bf16[256,3,16,128]{3,2,1,0:T(8,128)(2,1)S(1)}, u32[]{:S(2)}) copy-start(bf16[256,3,16,128]{3,2,1,0:T(8,128)(2,1)S(1)} %all-to-all-done) | copy-start | bytes 9437188

commit v2 on v1

v2 whole, which is shorter than its diff:
```python
import math

import jax
import jax.numpy as jnp
from jax import lax
from jax.experimental import pallas as pl
from jax.experimental.pallas import tpu as pltpu
from jax.sharding import PartitionSpec as P

F32 = jnp.float32
BF16 = jnp.bfloat16
SUB = 4
UNROLL = 2
PITCH = 200


def dot(a, b, dims):
    return lax.dot_general(a, b, (dims, ((), ())), preferred_element_type=F32)


def front_kernel(root_ref, loc_ref, lat_ref, ctrl_hbm, leg_hbm, out_hbm,
                 ctrl_ref, leg_ref, spec_scr, mix_scr, perm_scr, stage_scr, out_ref, ctrl_sem, leg_sem, out_sem):
    members = ctrl_ref.shape[0]
    slots, waves, lats = leg_ref.shape
    groups = lats // SUB
    dests = out_ref.shape[0]
    ctrl_in = [pltpu.make_async_copy(ctrl_hbm.at[k], ctrl_ref.at[k], ctrl_sem.at[k]) for k in range(members)]
    leg_in = [pltpu.make_async_copy(leg_hbm.at[s], leg_ref.at[s], leg_sem.at[s]) for s in range(slots)]
    for copy in ctrl_in + leg_in:
        copy.start()

    rows = lax.broadcasted_iota(jnp.int32, (32, 512), 0)
    lanes = lax.broadcasted_iota(jnp.int32, (32, 512), 1)
    pick_v = jnp.where(rows == lanes // 16, 1.0, 0.0).astype(BF16)
    spread = dot(root_ref[...].astype(BF16), pick_v, ((1,), (0,)))

    def mix_rows(h, carry):
        mix_scr[pl.ds(pl.multiple_of(h * 32, 32), 32), :] = jnp.where(lanes % 16 == h, spread, 0.0).astype(BF16)
        return carry

    lax.fori_loop(0, 16, mix_rows, 0)

    lat_row = jnp.broadcast_to(lat_ref[...].reshape(1, lats).astype(F32), (128, lats))
    stage_scr[0, pl.ds(0, lats), :] = jnp.transpose(lat_row)
    cols = lax.broadcasted_iota(jnp.int32, (groups, 128), 1).astype(F32)

    def pick_rows(a, carry):
        wanted = stage_scr[0, pl.ds(a, groups, stride=SUB), :]
        rows = pl.ds(pl.multiple_of(a * groups, 64), groups)
        for c in range(lats // 128):
            hit = jnp.where(cols + 128.0 * c == wanted, 1.0, 0.0).astype(BF16)
            perm_scr[rows, pl.ds(c * 128, 128)] = hit
        return carry

    lax.fori_loop(0, SUB, pick_rows, 0)

    def mix_member(k, carry):
        pltpu.make_async_copy(ctrl_hbm.at[k], ctrl_ref.at[k], ctrl_sem.at[k]).wait()
        mixed = dot(mix_scr[...], ctrl_ref[k].reshape(512, waves), ((1,), (0,))) * loc_ref[...]
        for r in range(2):
            for s in range(slots):
                for q in range(4):
                    src = (r * slots + s) * 32 + q * 8
                    rows = pl.ds(pl.multiple_of(q * 64 + r * 32 + k * 8, 8), 8)
                    spec_scr[s, rows, :] = mixed[src:src + 8]
        return carry

    lax.fori_loop(0, members, mix_member, 0)

    def one_slot(slot):
        spec = spec_scr[slot].astype(BF16)
        fourier = dot(spec, leg_ref[slot], ((1,), (0,))).astype(BF16)
        sorted_rows = dot(perm_scr[...], fourier, ((1,), (1,)))
        lane_group = lax.broadcasted_iota(jnp.int32, (groups, 128), 1) // 32
        for half in range(2):
            parts = [sorted_rows[a * groups:(a + 1) * groups, half * 128:(half + 1) * 128] for a in range(SUB)]
            turned = []
            for d in range(SUB):
                piece = parts[d]
                for p in range(1, SUB):
                    piece = jnp.where(lane_group == p, parts[(p + d) % SUB], piece)
                turned.append(pltpu.roll(piece, 32 * d, 1) if d else piece)
            for q in range(4):
                piece = turned[(0 - q) % SUB]
                for a in range(1, SUB):
                    piece = jnp.where(lane_group == a, turned[(a - q) % SUB], piece)
                stage_scr[half * 4 + q, pl.ds(pl.multiple_of(slot * PITCH, 8), groups), :] = piece

    def slot_step(step, carry):
        for u in range(UNROLL):
            slot = step * UNROLL + u
            pltpu.make_async_copy(leg_hbm.at[slot], leg_ref.at[slot], leg_sem.at[slot]).wait()
        for u in range(UNROLL):
            one_slot(step * UNROLL + u)
        return carry

    lax.fori_loop(0, slots // UNROLL, slot_step, 0)

    def emit(dest, carry):
        for third in range(3):
            for q in range(4):
                tiles = [stage_scr[q * 2 + r, pl.ds(dest * 3 + third, 8, stride=PITCH), :] for r in range(2)]
                out_ref[dest, q, third] = jnp.concatenate(tiles, axis=0).astype(BF16)
        return carry

    share = dests // 4

    def emit_part(part, carry):
        lax.fori_loop(part * share, (part + 1) * share, emit, 0)
        here = pl.ds(part * share, share)
        pltpu.make_async_copy(out_ref.at[here], out_hbm.at[here], out_sem.at[part]).start()
        return carry

    lax.fori_loop(0, 4, emit_part, 0)
    for part in range(4):
        here = pl.ds(part * share, share)
        pltpu.make_async_copy(out_ref.at[here], out_hbm.at[here], out_sem.at[part]).wait()


def front(control, vert_root, loc_spec, legendre, lat_order):
    members, levels, _, slots, waves = control.shape
    lats = legendre.shape[2]
    ctrl = control.reshape(members, levels, 2 * slots, waves)
    small = pl.BlockSpec(memory_space=pltpu.VMEM)
    far = pl.BlockSpec(memory_space=pltpu.HBM)
    out = (64, 4, 3, 16, 128)
    return pl.pallas_call(
        front_kernel,
        in_specs=[small, small, small, far, far],
        out_specs=far,
        out_shape=jax.ShapeDtypeStruct(out, BF16),
        scratch_shapes=[
            pltpu.VMEM(ctrl.shape, BF16),
            pltpu.VMEM(legendre.shape, BF16),
            pltpu.VMEM((slots, 256, waves), F32),
            pltpu.VMEM((512, 512), BF16),
            pltpu.VMEM((lats, lats), BF16),
            pltpu.VMEM((8, slots * PITCH, 128), F32),
            pltpu.VMEM(out, BF16),
            pltpu.SemaphoreType.DMA((members,)),
            pltpu.SemaphoreType.DMA((slots,)),
            pltpu.SemaphoreType.DMA((4,)),
        ],
        compiler_params=pltpu.CompilerParams(vmem_limit_bytes=60 * 1024 * 1024),
        name="front",
    )(vert_root, loc_spec.reshape(1, waves), lat_order, ctrl, legendre)


def make_basis(wave_table, lon_count):
    waves = wave_table.reshape(-1, 1, 8, 1)
    longitude = lax.iota(jnp.int32, lon_count)
    phases = waves * longitude % lon_count
    angles = phases.astype(F32) * (2.0 * math.pi / lon_count)
    weights = jnp.where(waves == 0, 1.0, 2.0).astype(F32)
    pair = jnp.concatenate([weights * jnp.cos(angles), -weights * jnp.sin(angles)], axis=1)
    return pair.astype(BF16).reshape(-1, lon_count)


COLS = 256


def back_kernel(recv_ref, basis_ref, ptb_ref, out_ref, turn_scr):
    @pl.when(pl.program_id(0) == 0)
    def _():
        for third in range(3):
            for q in range(4):
                coefs = recv_ref[:, q, third].reshape(1024, 128)
                turn_scr[third, pl.ds(q * 128, 128), :] = jnp.transpose(coefs)

    for third in range(3):
        field = dot(turn_scr[third], basis_ref[...], ((1,), (0,))).astype(BF16).astype(F32)
        field = field.reshape(4, SUB, 4, 8, COLS)
        for a in range(SUB):
            total = None
            for q in range(4):
                for k in range(4):
                    term = field[q, a, k] * ptb_ref[third * SUB + a, q * 4 + k].astype(F32)
                    total = term if total is None else total + term
            out_ref[third * SUB + a] = total.astype(BF16)


def back(recv, basis, perturb):
    lats, members, levels, lons = perturb.shape
    return pl.pallas_call(
        back_kernel,
        grid=(lons // COLS,),
        in_specs=[
            pl.BlockSpec(memory_space=pltpu.VMEM),
            pl.BlockSpec((1024, COLS), lambda c: (0, c)),
            pl.BlockSpec((lats, members, levels, COLS), lambda c: (0, 0, 0, c)),
        ],
        out_specs=pl.BlockSpec((lats, levels, COLS), lambda c: (0, 0, c)),
        out_shape=jax.ShapeDtypeStruct((lats, levels, lons), BF16),
        scratch_shapes=[pltpu.VMEM((3, 512, 1024), BF16)],
        compiler_params=pltpu.CompilerParams(vmem_limit_bytes=48 * 1024 * 1024),
        name="back",
    )(recv, basis, perturb)


def shards(control, vert_root, loc_spec, legendre, wave_table, lat_order, perturb):
    send = front(control, vert_root, loc_spec, legendre, lat_order)
    recv = lax.all_to_all(send.reshape(256, 3, 16, 128), ("rows", "mem"), 0, 0, tiled=True)
    basis = make_basis(wave_table, perturb.shape[3])
    return back(recv.reshape(64, 4, 3, 16, 128), basis, perturb)


def solution(mesh):
    return jax.shard_map(
        shards,
        mesh=mesh,
        in_specs=(
            P("mem", None, None, "rows", None),
            P(),
            P(),
            P("rows", None, None),
            P(),
            P(),
            P("rows", None, "mem", None),
        ),
        out_specs=P("rows", "mem", None),
        check_vma=False,
    )
```

time: 121 us -> 114 us (0.942)
  Pallas kernels: 25.8 us -> 22.1 us
  local copies, waits for them, and re-layouts: 3.31 us -> 0.09 us
    pallas_call x2, Pallas kernels: 25.8 us -> 22.1 us  [the longest x1 12.5 us: front(): pl.pallas_call(front_kernel, in_specs=[small, small, small, far, far], ou...]
    unnamed x4 -> x2, local copies, waits for them, and re-layouts: 1.67 us -> 0.01 us
    reshape x2 -> x0, local copies, waits for them, and re-layouts: 1.48 us -> none  [front(): lat_row = lat_order.reshape(lats // SUB, SUB).T.reshape(1, lats)]
  transfers between devices with their start and end apart: 1 -> 1, of which waited for: 1 -> 1; matrix products, arithmetic and copies ran while one was open for 13% -> 14% of each run, Pallas kernels for 0% -> 0%
where the time goes in v2:
time: 114 us
  waiting for transfers between devices  60.1 us (53%)
  Pallas kernels  22.1 us (19%)
  other arithmetic  15.8 us (14%)
  starting transfers between devices  15.7 us (14%)
    all_to_all x1, waiting for transfers between devices, shards(): lax.all_to_all(send.reshape(256, 3, 16, 128), ('rows', 'mem'), 0, 0, tile...  60.1 us
    all_to_all x1, starting transfers between devices, shards(): lax.all_to_all(send.reshape(256, 3, 16, 128), ('rows', 'mem'), 0, 0, tile...  15.7 us
    another operation x1, other arithmetic  13.8 us
    pallas_call x1, Pallas kernels, front(): pl.pallas_call(front_kernel, in_specs=[small, small, small, far, far], ou...  12.5 us
    pallas_call x1, Pallas kernels, back(): pl.pallas_call(back_kernel, grid=(lons // COLS,), in_specs=[pl.BlockSpec(...  9.61 us
  transfers between devices with their start and end apart: 1, of which 1 were waited for; matrix products, arithmetic and copies ran while one was open for 14% of the time, Pallas kernels for 0%

profile of v2, /device:TPU:1, one launch (start us, length us, event | category | flops | bytes accessed | tf_op | source)
XLA Modules:
  0.0 113.7 jit_solution(3711642628856255107)
XLA Ops:
  0.0 12.5 %front.1 = bf16[64,4,3,16,128]{4,3,2,1,0:T(8,128)(2,1)} custom-call(f32[32,32]{1,0:T(8,128)} %root_ref.1, f32[1,512]{1,0:T(1,128)} %bitcast.9, s32[768]{0:T(1024)} %lat_ref.1, bf16[4,32,16,512]{3,2,1,0:T(8,128)(2,1)} %bitcast.8, bf16[8,512,768]{2,1,0:T(8,128)(2,1)} %leg_hbm.1), custom_call_target="tpu_custom_call" | custom-call | tf_op jit(solution)/shard_map/front/pallas_call | solution.py:127
  12.5 0.0 copy-start
  12.5 15.7 %all-to-all-start = ((bf16[256,3,16,128]{3,2,1,0:T(8,128)(2,1)}), bf16[256,3,16,128]{3,2,1,0:T(8,128)(2,1)S(1)}, u32[]{:S(2)}, u32[]{:S(2)}) async-start(bf16[256,3,16,128]{3,2,1,0:T(8,128)(2,1)} %bitcast.6), calls=%async_computation | async-start | bytes 6291456 | tf_op jit(solution)/shard_map/all_to_all | solution.py:202
  28.1 0.0 copy-done
  28.2 0.1 reshape.99
  28.3 13.8 %multiply_convert_fusion.1 = (bf16[64,1,8,1536]{3,2,1,0:T(8,128)(2,1)S(1)}, bf16[64,1,8,1536]{3,2,1,0:T(8,128)(2,1)S(1)}) fusion(s32[64,8]{1,0:T(8,128)S(1)} %reshape.99, f32[64,8]{1,0:T(8,128)S(1)} %get-tuple-element.7, f32[64,8]{1,0:T(8,128)S(1)} %get-tuple-element.8), kind=kLoop, calls=%fused_computation.5 | loop fusion | flops 10223616 | bytes 3151872 | tf_op jit(solution)/shard_map/convert
  42.0 2.0 %pad_maximum_fusion = bf16[64,2,8,1536]{3,2,1,0:T(8,128)(2,1)} fusion(bf16[64,1,8,1536]{3,2,1,0:T(8,128)(2,1)S(1)} %get-tuple-element.6, bf16[64,1,8,1536]{3,2,1,0:T(8,128)(2,1)S(1)} %get-tuple-element.5), kind=kLoop, calls=%fused_computation.3 | loop fusion | flops 1572864 | bytes 6291456 | tf_op jit(solution)/shard_map/concatenate | solution.py:155
  44.0 60.1 %all-to-all-done = bf16[256,3,16,128]{3,2,1,0:T(8,128)(2,1)S(1)} async-done(((bf16[256,3,16,128]{3,2,1,0:T(8,128)(2,1)}), bf16[256,3,16,128]{3,2,1,0:T(8,128)(2,1)S(1)}, u32[]{:S(2)}, u32[]{:S(2)}) %all-to-all-start) | async-done | bytes 3145760 | tf_op jit(solution)/shard_map/all_to_all | solution.py:202
  104.1 9.6 %back.1 = bf16[12,8,1536]{2,1,0:T(8,128)(2,1)} custom-call(bf16[64,4,3,16,128]{4,3,2,1,0:T(8,128)(2,1)S(1)} %bitcast.5, bf16[1024,1536]{1,0:T(8,128)(2,1)} %bitcast.7, bf16[12,16,8,1536]{3,2,1,0:T(8,128)(2,1)} %ptb_ref.1), custom_call_target="tpu_custom_call" | custom-call | tf_op jit(solution)/shard_map/back/pallas_call | solution.py:184
  (1 shorter events, 0.0 us)
Async XLA Ops:
  12.5 15.7 %copy-start = (s32[512]{0:T(512)S(1)}, s32[512]{0:T(512)}, u32[]{:S(2)}) copy-start(s32[512]{0:T(512)} %param.11) | copy-start | bytes 6148
  12.5 91.6 %all-to-all-start = ((bf16[256,3,16,128]{3,2,1,0:T(8,128)(2,1)}), bf16[256,3,16,128]{3,2,1,0:T(8,128)(2,1)S(1)}, u32[]{:S(2)}, u32[]{:S(2)}) async-start(bf16[256,3,16,128]{3,2,1,0:T(8,128)(2,1)} %bitcast.6), calls=%async_computation | async-start | bytes 6291456 | tf_op jit(solution)/shard_map/all_to_all | solution.py:202

commit v3 on v2

v3 whole, which is shorter than its diff:
```python
import functools
import math

import jax
import jax.numpy as jnp
from jax import lax
from jax.experimental import pallas as pl
from jax.experimental.pallas import tpu as pltpu
from jax.sharding import Mesh
from jax.sharding import PartitionSpec as P

F32 = jnp.float32
BF16 = jnp.bfloat16
SUB = 4
UNROLL = 2
PITCH = 200
NZ = 8


def dot(a, b, dims):
    return lax.dot_general(a, b, (dims, ((), ())), preferred_element_type=F32)


def front_kernel(z_ref, root_ref, loc_ref, lat_ref, ctrl_hbm, leg_hbm, *rest):
    outs_hbm = rest[:10]
    (ctrl_ref, leg_ref, spec_scr, mix_scr, perm_scr, stage_scr) = rest[10:16]
    out_refs = rest[16:26]
    ctrl_sem, leg_sem, out_sem = rest[26:]
    members = ctrl_ref.shape[0]
    slots, waves, lats = leg_ref.shape
    groups = lats // SUB
    ctrl_in = [pltpu.make_async_copy(ctrl_hbm.at[k], ctrl_ref.at[k], ctrl_sem.at[k]) for k in range(members)]
    leg_in = [pltpu.make_async_copy(leg_hbm.at[s], leg_ref.at[s], leg_sem.at[s]) for s in range(slots)]
    for copy in ctrl_in + leg_in:
        copy.start()

    rows = lax.broadcasted_iota(jnp.int32, (32, 512), 0)
    lanes = lax.broadcasted_iota(jnp.int32, (32, 512), 1)
    pick_v = jnp.where(rows == lanes // 16, 1.0, 0.0).astype(BF16)
    spread = dot(root_ref[...].astype(BF16), pick_v, ((1,), (0,)))

    def mix_rows(h, carry):
        mix_scr[pl.ds(pl.multiple_of(h * 32, 32), 32), :] = jnp.where(lanes % 16 == h, spread, 0.0).astype(BF16)
        return carry

    lax.fori_loop(0, 16, mix_rows, 0)

    lat_row = jnp.broadcast_to(lat_ref[...].reshape(1, lats).astype(F32), (128, lats))
    stage_scr[0, pl.ds(0, lats), :] = jnp.transpose(lat_row)
    cols = lax.broadcasted_iota(jnp.int32, (groups, 128), 1).astype(F32)

    def pick_rows(a, carry):
        wanted = stage_scr[0, pl.ds(a, groups, stride=SUB), :]
        rows = pl.ds(pl.multiple_of(a * groups, 64), groups)
        for c in range(lats // 128):
            hit = jnp.where(cols + 128.0 * c == wanted, 1.0, 0.0).astype(BF16)
            perm_scr[rows, pl.ds(c * 128, 128)] = hit
        return carry

    lax.fori_loop(0, SUB, pick_rows, 0)

    def mix_member(k, carry):
        pltpu.make_async_copy(ctrl_hbm.at[k], ctrl_ref.at[k], ctrl_sem.at[k]).wait()
        mixed = dot(mix_scr[...], ctrl_ref[k].reshape(512, waves), ((1,), (0,))) * loc_ref[...]
        for r in range(2):
            for s in range(slots):
                for q in range(4):
                    src = (r * slots + s) * 32 + q * 8
                    rows = pl.ds(pl.multiple_of(q * 64 + r * 32 + k * 8, 8), 8)
                    spec_scr[s, rows, :] = mixed[src:src + 8]
        return carry

    lax.fori_loop(0, members, mix_member, 0)

    def one_slot(slot):
        spec = spec_scr[slot].astype(BF16)
        fourier = dot(spec, leg_ref[slot], ((1,), (0,))).astype(BF16)
        sorted_rows = dot(perm_scr[...], fourier, ((1,), (1,)))
        lane_group = lax.broadcasted_iota(jnp.int32, (groups, 128), 1) // 32
        for half in range(2):
            parts = [sorted_rows[a * groups:(a + 1) * groups, half * 128:(half + 1) * 128] for a in range(SUB)]
            turned = []
            for d in range(SUB):
                piece = parts[d]
                for p in range(1, SUB):
                    piece = jnp.where(lane_group == p, parts[(p + d) % SUB], piece)
                turned.append(pltpu.roll(piece, 32 * d, 1) if d else piece)
            for q in range(4):
                piece = turned[(0 - q) % SUB]
                for a in range(1, SUB):
                    piece = jnp.where(lane_group == a, turned[(a - q) % SUB], piece)
                stage_scr[half * 4 + q, pl.ds(pl.multiple_of(slot * PITCH, 8), groups), :] = piece

    def slot_step(step, carry):
        for u in range(UNROLL):
            slot = step * UNROLL + u
            pltpu.make_async_copy(leg_hbm.at[slot], leg_ref.at[slot], leg_sem.at[slot]).wait()
        for u in range(UNROLL):
            one_slot(step * UNROLL + u)
        return carry

    lax.fori_loop(0, slots // UNROLL, slot_step, 0)

    def tile(q, dest, third):
        tiles = [stage_scr[q * 2 + r, pl.ds(dest * 3 + third, 8, stride=PITCH), :] for r in range(2)]
        return jnp.concatenate(tiles, axis=0).astype(BF16)

    def send(n):
        return pltpu.make_async_copy(out_refs[n], outs_hbm[n], out_sem.at[n])

    def emit_planes(third, peer, carry):
        for dz in range(NZ):
            dest = (z_ref[0] + dz) % NZ * 8 + peer
            for q in range(4):
                out_refs[7 + third][peer * 4 + q, dz] = tile(q, dest, third)
        return carry

    def emit_hops(peer, carry):
        for dz in range(NZ):
            dest = (z_ref[0] + dz) % NZ * 8 + peer
            for q in range(4):
                out_refs[dz][peer * 4 + q] = tile(q, dest, 0)
        return carry

    for third in (1, 2):
        lax.fori_loop(0, 8, functools.partial(emit_planes, third), 0)
        send(7 + third).start()
    lax.fori_loop(0, 8, emit_hops, 0)
    for dz in range(NZ):
        send(dz).start()
    for n in range(10):
        send(n).wait()


def front(place, control, vert_root, loc_spec, legendre, lat_order):
    members, levels, _, slots, waves = control.shape
    lats = legendre.shape[2]
    ctrl = control.reshape(members, levels, 2 * slots, waves)
    small = pl.BlockSpec(memory_space=pltpu.VMEM)
    far = pl.BlockSpec(memory_space=pltpu.HBM)
    outs = [(32, 16, 128)] * NZ + [(32, NZ, 16, 128)] * 2
    return pl.pallas_call(
        front_kernel,
        in_specs=[pl.BlockSpec(memory_space=pltpu.SMEM), small, small, small, far, far],
        out_specs=[far] * 10,
        out_shape=[jax.ShapeDtypeStruct(out, BF16) for out in outs],
        scratch_shapes=[
            pltpu.VMEM(ctrl.shape, BF16),
            pltpu.VMEM(legendre.shape, BF16),
            pltpu.VMEM((slots, 256, waves), F32),
            pltpu.VMEM((512, 512), BF16),
            pltpu.VMEM((lats, lats), BF16),
            pltpu.VMEM((8, slots * PITCH, 128), F32),
            *[pltpu.VMEM(out, BF16) for out in outs],
            pltpu.SemaphoreType.DMA((members,)),
            pltpu.SemaphoreType.DMA((slots,)),
            pltpu.SemaphoreType.DMA((10,)),
        ],
        compiler_params=pltpu.CompilerParams(vmem_limit_bytes=60 * 1024 * 1024),
        name="front",
    )(place, vert_root, loc_spec.reshape(1, waves), lat_order, ctrl, legendre)


BAND = 64


def basis_kernel(wave_ref, out_ref):
    lons = out_ref.shape[1]
    lanes = lax.broadcasted_iota(jnp.int32, (BAND, 128), 1).astype(F32)
    step = 2.0 * math.pi / lons

    def wrap(count, period):
        return count - period * jnp.floor((count + 0.5) * (1.0 / period))

    def band(i, carry):
        wave = wave_ref[pl.ds(pl.multiple_of(i * BAND, BAND), BAND), :]
        count = wave * lanes
        near = wrap(count, float(lons)) * step
        far = wrap(count, lons / 128.0) * (128.0 * step)
        weight = jnp.where(wave == 0.0, 1.0, 2.0)
        near_cos, near_sin = weight * jnp.cos(near), weight * jnp.sin(near)
        far_cos, far_sin = jnp.cos(far), jnp.sin(far)
        for b in range(lons // 128):
            c, s = far_cos[:, b:b + 1], far_sin[:, b:b + 1]
            real = c * near_cos - s * near_sin
            imag = -(s * near_cos + c * near_sin)
            for row in range(BAND // 8):
                cut = slice(row * 8, row * 8 + 8)
                both = jnp.concatenate([real[cut], imag[cut]], axis=0).astype(BF16)
                out_ref[pl.ds(pl.multiple_of(i * 2 * BAND + row * 16, 16), 16), pl.ds(b * 128, 128)] = both
        return carry

    lax.fori_loop(0, wave_ref.shape[0] // BAND, band, 0)


def make_basis(wave_table, lon_count):
    waves = wave_table.shape[0]
    return pl.pallas_call(
        basis_kernel,
        out_shape=jax.ShapeDtypeStruct((2 * waves, lon_count), BF16),
        compiler_params=pltpu.CompilerParams(vmem_limit_bytes=48 * 1024 * 1024),
        name="basis",
    )(jnp.broadcast_to(wave_table.astype(F32)[:, None], (waves, 128)))


def stack_kernel(*refs):
    for dz in range(NZ):
        refs[NZ][:, dz] = refs[dz][...]


def stack(blocks):
    near = pl.BlockSpec(memory_space=pltpu.VMEM)
    return pl.pallas_call(
        stack_kernel,
        in_specs=[near] * NZ,
        out_specs=near,
        out_shape=jax.ShapeDtypeStruct((32, NZ, 16, 128), BF16),
        compiler_params=pltpu.CompilerParams(vmem_limit_bytes=48 * 1024 * 1024),
        name="stack",
    )(*blocks)


COLS = 512


def back_kernel(*refs, counts):
    total_refs = sum(counts)
    recv_refs, (basis_ref, ptb_ref), (out_ref, turn_scr) = refs[:total_refs], refs[total_refs:total_refs + 2], refs[-2:]

    @pl.when(pl.program_id(0) == 0)
    def _():
        first = 0
        for t, count in enumerate(counts):
            for q in range(4):
                for dz in range(NZ):
                    coefs = recv_refs[first][:, q, dz] if count == 1 else recv_refs[first + dz][:, q]
                    turn_scr[t, pl.ds(q * 128, 128), pl.ds(dz * 128, 128)] = jnp.transpose(coefs.reshape(128, 128))
            first += count

    width = 256
    for c in range(COLS // width):
        cols = pl.ds(c * width, width)
        for t in range(len(counts)):
            field = dot(turn_scr[t], basis_ref[:, cols], ((1,), (0,))).astype(BF16).astype(F32)
            field = field.reshape(4, SUB, 4, 8, width)
            for a in range(SUB):
                total = None
                for q in range(4):
                    for k in range(4):
                        term = field[q, a, k] * ptb_ref[t * SUB + a, q * 4 + k, :, cols].astype(F32)
                        total = term if total is None else total + term
                out_ref[t * SUB + a, :, cols] = total.astype(BF16)


def back(groups, basis, perturb, block, done):
    lats, members, levels, lons = perturb.shape
    counts = tuple(len(pieces) for pieces in groups)
    rows = SUB * len(groups)
    args = []
    for pieces in groups:
        shape = (8, 4, NZ, 16, 128) if len(pieces) == 1 else (8, 4, 16, 128)
        args += [piece.reshape(shape) for piece in pieces]
    specs = [pl.BlockSpec(memory_space=pltpu.VMEM)] * len(args) + [
        pl.BlockSpec((1024, COLS), lambda c: (0, c)),
        pl.BlockSpec((rows, members, levels, COLS), lambda c: (block, 0, 0, c)),
    ]
    args += [basis, perturb]
    aliases = {}
    if done is not None:
        aliases = {len(args): 0}
        specs.append(pl.BlockSpec(memory_space=pl.ANY))
        args.append(done)
    return pl.pallas_call(
        functools.partial(back_kernel, counts=counts),
        grid=(lons // COLS,),
        in_specs=specs,
        out_specs=pl.BlockSpec((rows, levels, COLS), lambda c: (block, 0, c)),
        out_shape=jax.ShapeDtypeStruct((lats, levels, lons), BF16),
        scratch_shapes=[pltpu.VMEM((len(groups), 512, 1024), BF16)],
        input_output_aliases=aliases,
        compiler_params=pltpu.CompilerParams(vmem_limit_bytes=48 * 1024 * 1024),
        name="back",
    )(*args)


def hop(blocks):
    moved = [blocks[0]]
    for dz in range(1, NZ):
        moved.append(lax.ppermute(blocks[dz], "z", [(i, (i + dz) % NZ) for i in range(NZ)]))
    return moved


def planes(block):
    return [block[:, dz] for dz in range(NZ)]


def plane(block):
    return lax.all_to_all(block, ("y", "c", "mem"), 0, 0, tiled=True)


def shards(control, vert_root, loc_spec, legendre, wave_table, lat_order, perturb):
    place = lax.axis_index("z")
    sends = front(place.reshape(1), control, vert_root, loc_spec, legendre, lat_order)
    table = jnp.roll(jnp.flip(wave_table.reshape(NZ, -1), 0), place + 1, 0)
    basis = make_basis(table.reshape(-1), perturb.shape[3])
    one = plane(sends[8])
    zero = hop(sends[:8])
    two = plane(sends[9])
    one = hop(planes(one))
    two = hop(planes(two))
    zero = stack(zero)
    zero = plane(zero)
    done = back([[zero], one], basis, perturb, 0, None)
    return back([two], basis, perturb, 2, done)


def solution(mesh):
    split = Mesh(mesh.devices.reshape(NZ, 4, 2, 4), ("z", "y", "c", "mem"))
    rows = ("z", "y", "c")
    return jax.shard_map(
        shards,
        mesh=split,
        in_specs=(
            P("mem", None, None, rows, None),
            P(),
            P(),
            P(rows, None, None),
            P(),
            P(),
            P(rows, None, "mem", None),
        ),
        out_specs=P(rows, "mem", None),
        check_vma=False,
    )
```

time: 114 us -> 159 us (1.39)
  the two profiles are of different devices: /device:TPU:1 before, /device:TPU:2 now
where the time goes in v3:
time: 159 us; the launch traced here: 158 us
  starting transfers between devices  68.9 us (43%)
  Pallas kernels  29.7 us (19%)
  waiting for transfers between devices  24.4 us (15%)
  blocking collectives  22.2 us (14%)
  local copies, waits for them, and re-layouts  12.9 us (8%)
    ppermute x21, starting transfers between devices, hop(): lax.ppermute(blocks[dz], 'z', [(i, (i + dz) % NZ) for i in range(NZ)])  54.9 us
    ppermute x21, waiting for transfers between devices, hop(): lax.ppermute(blocks[dz], 'z', [(i, (i + dz) % NZ) for i in range(NZ)])  24.4 us
    all_to_all x1, blocking collectives, plane(): return lax.all_to_all(block, ('y', 'c', 'mem'), 0, 0, tiled=True)  22.2 us
    all_to_all x2, starting transfers between devices, plane(): return lax.all_to_all(block, ('y', 'c', 'mem'), 0, 0, tiled=True)  14.1 us
    pallas_call x1, Pallas kernels, front(): pl.pallas_call(front_kernel, in_specs=[pl.BlockSpec(memory_space=pltpu.SM...  13.1 us
    pallas_call x2, Pallas kernels, back(): pl.pallas_call(functools.partial(back_kernel, counts=counts), grid=(lons...  11.9 us
    unnamed x36, local copies, waits for them, and re-layouts  11.5 us
    pallas_call x1, Pallas kernels, make_basis(): pl.pallas_call(basis_kernel, out_shape=jax.ShapeDtypeStruct((2 * waves, l...  3.64 us
  transfers between devices with their start and end apart: 23, of which 8 were waited for; matrix products, arithmetic and copies ran while one was open for 1% of the time, Pallas kernels for 7%

profile of v3, /device:TPU:2, one launch (start us, length us, event | category | flops | bytes accessed | tf_op | source)
XLA Modules:
  0.0 158.4 jit_solution(17301977588773286004)
XLA Ops:
  0.0 13.1 %front.1 = (bf16[32,16,128]{2,1,0:T(8,128)(2,1)}, bf16[32,16,128]{2,1,0:T(8,128)(2,1)}, bf16[32,16,128]{2,1,0:T(8,128)(2,1)}, bf16[32,16,128]{2,1,0:T(8,128)(2,1...) custom-call(s32[1]{0:T(128)} %bitcast.z_ref, ...), custom_call_target="tpu_custom_call" | custom-call | tf_op jit(solution)/shard_map/front/pallas_call | solution.py:142
  13.1 22.2 %all_to_all.15 = bf16[32,8,16,128]{3,2,1,0:T(8,128)(2,1)S(1)} all-to-all(bf16[32,8,16,128]{3,2,1,0:T(8,128)(2,1)} %get-tuple-element.15), channel_id=1, replica_groups=mesh['z'=8,'y'=4,'c'=2,'mem'=4] {'y','c','mem'}, dimensions={0} | all-to-all | bytes 2097152 | tf_op jit(solution)/shard_map/all_to_all | solution.py:298
  35.3 6.6 %all-to-all-start.2 = ((bf16[32,8,16,128]{3,2,1,0:T(8,128)(2,1)}), bf16[32,8,16,128]{3,2,1,0:T(8,128)(2,1)S(1)}, u32[]{:S(2)}, u32[]{:S(2)}) async-start(bf16[32,8,16,128]{3,2,1,0:T(8,128)(2,1)} %get-tuple-element.24), calls=%async_computation.2 | async-start | bytes 2097152 | tf_op jit(solution)/shard_map/all_to_all | solution.py:298
  42.0 2.0 %collective-permute-start.7 = (bf16[32,16,128]{2,1,0:T(8,128)(2,1)}, bf16[32,16,128]{2,1,0:T(8,128)(2,1)S(1)}, u32[]{:S(2)}, u32[]{:S(2)}) collective-permute-start(bf16[32,16,128]{2,1,0:T(8,128)(2,1)} %get-tuple-element.17), channel_id=1, source_target_pairs={{0,32},{32,64},{64,96},{96,128},{128,160},{160,192},{192,224},{224... | collective-permute-start | bytes 393224 | tf_op jit(solution)/shard_map/ppermute | solution.py:289
  44.0 3.3 %collective-permute-start.8 = (bf16[32,16,128]{2,1,0:T(8,128)(2,1)}, bf16[32,16,128]{2,1,0:T(8,128)(2,1)S(1)}, u32[]{:S(2)}, u32[]{:S(2)}) collective-permute-start(bf16[32,16,128]{2,1,0:T(8,128)(2,1)} %get-tuple-element.18), channel_id=1, source_target_pairs={{0,64},{32,96},{64,128},{96,160},{128,192},{160,224},{192,0},{224,... | collective-permute-start | bytes 393224 | tf_op jit(solution)/shard_map/ppermute | solution.py:289
  47.3 4.0 %collective-permute-start.9 = (bf16[32,16,128]{2,1,0:T(8,128)(2,1)}, bf16[32,16,128]{2,1,0:T(8,128)(2,1)S(1)}, u32[]{:S(2)}, u32[]{:S(2)}) collective-permute-start(bf16[32,16,128]{2,1,0:T(8,128)(2,1)} %get-tuple-element.19), channel_id=1, source_target_pairs={{0,96},{32,128},{64,160},{96,192},{128,224},{160,0},{192,32},{224,... | collective-permute-start | bytes 393224 | tf_op jit(solution)/shard_map/ppermute | solution.py:289
  51.8 4.9 %collective-permute-start.11 = (bf16[32,16,128]{2,1,0:T(8,128)(2,1)}, bf16[32,16,128]{2,1,0:T(8,128)(2,1)S(1)}, u32[]{:S(2)}, u32[]{:S(2)}) collective-permute-start(bf16[32,16,128]{2,1,0:T(8,128)(2,1)} %get-tuple-element.21), channel_id=1, source_target_pairs={{0,160},{32,192},{64,224},{96,0},{128,32},{160,64},{192,96},{224,1... | collective-permute-start | bytes 393224 | tf_op jit(solution)/shard_map/ppermute | solution.py:289
  56.8 2.7 %collective-permute-start.12 = (bf16[32,16,128]{2,1,0:T(8,128)(2,1)}, bf16[32,16,128]{2,1,0:T(8,128)(2,1)S(1)}, u32[]{:S(2)}, u32[]{:S(2)}) collective-permute-start(bf16[32,16,128]{2,1,0:T(8,128)(2,1)} %get-tuple-element.22), channel_id=1, source_target_pairs={{0,192},{32,224},{64,0},{96,32},{128,64},{160,96},{192,128},{224,1... | collective-permute-start | bytes 393224 | tf_op jit(solution)/shard_map/ppermute | solution.py:289
  59.4 1.1 collective-permute-done.8.refs_2_
  60.5 3.3 %collective-permute-start.13 = (bf16[32,16,128]{2,1,0:T(8,128)(2,1)}, bf16[32,16,128]{2,1,0:T(8,128)(2,1)S(1)}, u32[]{:S(2)}, u32[]{:S(2)}) collective-permute-start(bf16[32,16,128]{2,1,0:T(8,128)(2,1)} %get-tuple-element.23), channel_id=1, source_target_pairs={{0,224},{32,0},{64,32},{96,64},{128,96},{160,128},{192,160},{224,1... | collective-permute-start | bytes 393224 | tf_op jit(solution)/shard_map/ppermute | solution.py:289
  63.9 5.4 %collective-permute-done.9.refs_3_ = bf16[32,16,128]{2,1,0:T(8,128)(2,1)S(1)} collective-permute-done((bf16[32,16,128]{2,1,0:T(8,128)(2,1)}, bf16[32,16,128]{2,1,0:T(8,128)(2,1)S(1)}, u32[]{:S(2)}, u32[]{:S(2)}) %collective-permute-start.9) | collective-permute-done | bytes 131104 | tf_op jit(solution)/shard_map/ppermute | solution.py:289
  69.3 3.3 %collective-permute-done.11.refs_5_ = bf16[32,16,128]{2,1,0:T(8,128)(2,1)S(1)} collective-permute-done((bf16[32,16,128]{2,1,0:T(8,128)(2,1)}, bf16[32,16,128]{2,1,0:T(8,128)(2,1)S(1)}, u32[]{:S(2)}, u32[]{:S(2)}) %collective-permute-start.11) | collective-permute-done | bytes 131104 | tf_op jit(solution)/shard_map/ppermute | solution.py:289
  72.5 3.4 %collective-permute-done.12.refs_6_ = bf16[32,16,128]{2,1,0:T(8,128)(2,1)S(1)} collective-permute-done((bf16[32,16,128]{2,1,0:T(8,128)(2,1)}, bf16[32,16,128]{2,1,0:T(8,128)(2,1)S(1)}, u32[]{:S(2)}, u32[]{:S(2)}) %collective-permute-start.12) | collective-permute-done | bytes 131104 | tf_op jit(solution)/shard_map/ppermute | solution.py:289
  75.9 0.7 collective-permute-done.13.refs_7_
  76.6 0.9 copy-done.16
  77.5 1.1 stack.1
  78.6 7.4 %all-to-all-start.1 = ((bf16[32,8,16,128]{3,2,1,0:T(8,128)(2,1)}), bf16[32,8,16,128]{3,2,1,0:T(8,128)(2,1)}, u32[]{:S(2)}, u32[]{:S(2)}) async-start(bf16[32,8,16,128]{3,2,1,0:T(8,128)(2,1)} %stack.1), calls=%async_computation.1 | async-start | bytes 2097152 | tf_op jit(solution)/shard_map/all_to_all | solution.py:298
  86.2 2.7 %collective-permute-start.20 = (bf16[32,16,128]{2,1,0:T(8,128)(2,1)S(1)}, bf16[32,16,128]{2,1,0:T(8,128)(2,1)S(1)}, u32[]{:S(2)}, u32[]{:S(2)}) collective-permute-start(bf16[32,16,128]{2,1,0:T(8,128)(2,1)S(1)} %get-tuple-element.25), channel_id=1, source_target_pairs={{0,224},{32,0},{64,32},{96,64},{128,96},{160,128},{192,160},{224,1... | collective-permute-start | bytes 393224 | tf_op jit(solution)/shard_map/ppermute | solution.py:289
  89.0 0.9 collective-permute-start.19
  89.9 3.8 %collective-permute-start.18 = (bf16[32,16,128]{2,1,0:T(8,128)(2,1)S(1)}, bf16[32,16,128]{2,1,0:T(8,128)(2,1)S(1)}, u32[]{:S(2)}, u32[]{:S(2)}) collective-permute-start(bf16[32,16,128]{2,1,0:T(8,128)(2,1)S(1)} %get-tuple-element.27), channel_id=1, source_target_pairs={{0,160},{32,192},{64,224},{96,0},{128,32},{160,64},{192,96},{224,1... | collective-permute-start | bytes 393224 | tf_op jit(solution)/shard_map/ppermute | solution.py:289
  93.8 1.2 collective-permute-start.17
  95.0 3.5 %collective-permute-start.16 = (bf16[32,16,128]{2,1,0:T(8,128)(2,1)S(1)}, bf16[32,16,128]{2,1,0:T(8,128)(2,1)S(1)}, u32[]{:S(2)}, u32[]{:S(2)}) collective-permute-start(bf16[32,16,128]{2,1,0:T(8,128)(2,1)S(1)} %get-tuple-element.29), channel_id=1, source_target_pairs={{0,96},{32,128},{64,160},{96,192},{128,224},{160,0},{192,32},{224,... | collective-permute-start | bytes 393224 | tf_op jit(solution)/shard_map/ppermute | solution.py:289
  98.5 0.9 slice_bitcast_fusion.7
  99.4 2.4 %collective-permute-start.15 = (bf16[32,16,128]{2,1,0:T(8,128)(2,1)S(1)}, bf16[32,16,128]{2,1,0:T(8,128)(2,1)S(1)}, u32[]{:S(2)}, u32[]{:S(2)}) collective-permute-start(bf16[32,16,128]{2,1,0:T(8,128)(2,1)S(1)} %get-tuple-element.30), channel_id=1, source_target_pairs={{0,64},{32,96},{64,128},{96,160},{128,192},{160,224},{192,0},{224,... | collective-permute-start | bytes 393224 | tf_op jit(solution)/shard_map/ppermute | solution.py:289
  101.8 3.7 %collective-permute-done.19 = bf16[32,16,128]{2,1,0:T(8,128)(2,1)S(1)} collective-permute-done((bf16[32,16,128]{2,1,0:T(8,128)(2,1)S(1)}, bf16[32,16,128]{2,1,0:T(8,128)(2,1)S(1)}, u32[]{:S(2)}, u32[]{:S(2)}) %collective-permute-start.19) | collective-permute-done | bytes 131104 | tf_op jit(solution)/shard_map/ppermute | solution.py:289
  105.5 0.6 copy-done
  106.5 0.7 copy-done.2
  107.2 6.9 %collective-permute-start.6 = (bf16[32,16,128]{2,1,0:T(8,128)(2,1)S(1)}, bf16[32,16,128]{2,1,0:T(8,128)(2,1)S(1)}, u32[]{:S(2)}, u32[]{:S(2)}) collective-permute-start(bf16[32,16,128]{2,1,0:T(8,128)(2,1)S(1)} %get-tuple-element.33), channel_id=1, source_target_pairs={{0,224},{32,0},{64,32},{96,64},{128,96},{160,128},{192,160},{224,1... | collective-permute-start | bytes 393224 | tf_op jit(solution)/shard_map/ppermute | solution.py:289
  114.0 0.6 copy-done.4
  114.7 1.1 collective-permute-start.5
  115.8 0.6 copy-done.6
  116.5 3.0 %collective-permute-start.4 = (bf16[32,16,128]{2,1,0:T(8,128)(2,1)}, bf16[32,16,128]{2,1,0:T(8,128)(2,1)}, u32[]{:S(2)}, u32[]{:S(2)}) collective-permute-start(bf16[32,16,128]{2,1,0:T(8,128)(2,1)} %get-tuple-element.35), channel_id=1, source_target_pairs={{0,160},{32,192},{64,224},{96,0},{128,32},{160,64},{192,96},{224,1... | collective-permute-start | bytes 393224 | tf_op jit(solution)/shard_map/ppermute | solution.py:289
  119.5 0.6 copy-done.12
  120.1 4.6 %collective-permute-start.3 = (bf16[32,16,128]{2,1,0:T(8,128)(2,1)}, bf16[32,16,128]{2,1,0:T(8,128)(2,1)}, u32[]{:S(2)}, u32[]{:S(2)}) collective-permute-start(bf16[32,16,128]{2,1,0:T(8,128)(2,1)} %get-tuple-element.36), channel_id=1, source_target_pairs={{0,128},{32,160},{64,192},{96,224},{128,0},{160,32},{192,64},{224,... | collective-permute-start | bytes 393224 | tf_op jit(solution)/shard_map/ppermute | solution.py:289
  124.7 0.7 copy-done.14
  125.4 3.8 %collective-permute-start.2 = (bf16[32,16,128]{2,1,0:T(8,128)(2,1)}, bf16[32,16,128]{2,1,0:T(8,128)(2,1)}, u32[]{:S(2)}, u32[]{:S(2)}) collective-permute-start(bf16[32,16,128]{2,1,0:T(8,128)(2,1)} %get-tuple-element.37), channel_id=1, source_target_pairs={{0,96},{32,128},{64,160},{96,192},{128,224},{160,0},{192,32},{224,... | collective-permute-start | bytes 393224 | tf_op jit(solution)/shard_map/ppermute | solution.py:289
  129.2 0.7 copy-done.8
  129.9 6.5 %collective-permute-done.5 = bf16[32,16,128]{2,1,0:T(8,128)(2,1)S(1)} collective-permute-done((bf16[32,16,128]{2,1,0:T(8,128)(2,1)S(1)}, bf16[32,16,128]{2,1,0:T(8,128)(2,1)S(1)}, u32[]{:S(2)}, u32[]{:S(2)}) %collective-permute-start.5) | collective-permute-done | bytes 131104 | tf_op jit(solution)/shard_map/ppermute | solution.py:289
  136.4 0.6 copy-done.10
  137.3 3.6 %basis.1.refs_9_.refs_8_ = bf16[1024,1536]{1,0:T(8,128)(2,1)S(1)} custom-call(f32[512,128]{1,0:T(8,128)S(1)} %broadcast_in_dim.2.wave_ref), custom_call_target="tpu_custom_call" | custom-call | tf_op jit(solution)/shard_map/basis/pallas_call | solution.py:198
  141.0 0.9 copy-done.1
  141.9 0.9 copy-done.3
  142.8 0.9 copy-done.5
  143.7 0.9 copy-done.7
  144.6 0.9 copy-done.13
  145.5 0.9 copy-done.15
  146.4 7.0 %back.2.refs_10_ = bf16[12,8,1536]{2,1,0:T(8,128)(2,1)} custom-call(bf16[8,4,8,16,128]{4,3,2,1,0:T(8,128)(2,1)} %bitcast.18.refs_0_, bf16[8,4,16,128]{3,2,1,0:T(8,128)(2,1)S(1)} %bitcast.48, bf16[8,4,16,128]{3,2,1,0:T(8,128)(2,1)S(1)} %bitcast.58, bf16[8,4,16,128]{3,2,1,0:T(8,128)(2,1)S(1)} %bitcast.57, bf16[8,4,16,128]{3,2,1,0:T(8,128)(2,1)S(1)} %bitcast.54, ...), custom_call_target="tpu_custom_call" | custom-call | tf_op jit(solution)/shard_map/back/pallas_call | solution.py:273
  153.5 4.9 %back.3 = bf16[12,8,1536]{2,1,0:T(8,128)(2,1)} custom-call(bf16[8,4,16,128]{3,2,1,0:T(8,128)(2,1)S(1)} %bitcast.49, bf16[8,4,16,128]{3,2,1,0:T(8,128)(2,1)} %bitcast.5.refs_1_, bf16[8,4,16,128]{3,2,1,0:T(8,128)(2,1)} %bitcast.7.refs_2_, bf16[8,4,16,128]{3,2,1,0:T(8,128)(2,1)} %bitcast.9.refs_3_, ...), custom_call_target="tpu_custom_call", output_to_operand_aliasing={{}: (10, {})} | custom-call | tf_op jit(solution)/shard_map/back/pallas_call | solution.py:273
  (47 shorter events, 1.5 us)
Async XLA Ops:
  35.3 43.3 %all-to-all-start.2 = ((bf16[32,8,16,128]{3,2,1,0:T(8,128)(2,1)}), bf16[32,8,16,128]{3,2,1,0:T(8,128)(2,1)S(1)}, u32[]{:S(2)}, u32[]{:S(2)}) async-start(bf16[32,8,16,128]{3,2,1,0:T(8,128)(2,1)} %get-tuple-element.24), calls=%async_computation.2 | async-start | bytes 2097152 | tf_op jit(solution)/shard_map/all_to_all | solution.py:298
  42.0 95.1 %copy-start.17 = (s32[512]{0:T(512)S(1)}, s32[512]{0:T(512)}, u32[]{:S(2)}) copy-start(s32[512]{0:T(512)} %param.11) | copy-start | bytes 6148
  42.0 14.8 %collective-permute-start.7 = (bf16[32,16,128]{2,1,0:T(8,128)(2,1)}, bf16[32,16,128]{2,1,0:T(8,128)(2,1)S(1)}, u32[]{:S(2)}, u32[]{:S(2)}) collective-permute-start(bf16[32,16,128]{2,1,0:T(8,128)(2,1)} %get-tuple-element.17), channel_id=1, source_target_pairs={{0,32},{32,64},{64,96},{96,128},{128,160},{160,192},{192,224},{224... | collective-permute-start | bytes 393224 | tf_op jit(solution)/shard_map/ppermute | solution.py:289
  44.0 16.6 %collective-permute-start.8 = (bf16[32,16,128]{2,1,0:T(8,128)(2,1)}, bf16[32,16,128]{2,1,0:T(8,128)(2,1)S(1)}, u32[]{:S(2)}, u32[]{:S(2)}) collective-permute-start(bf16[32,16,128]{2,1,0:T(8,128)(2,1)} %get-tuple-element.18), channel_id=1, source_target_pairs={{0,64},{32,96},{64,128},{96,160},{128,192},{160,224},{192,0},{224,... | collective-permute-start | bytes 393224 | tf_op jit(solution)/shard_map/ppermute | solution.py:289
  47.3 22.0 %collective-permute-start.9 = (bf16[32,16,128]{2,1,0:T(8,128)(2,1)}, bf16[32,16,128]{2,1,0:T(8,128)(2,1)S(1)}, u32[]{:S(2)}, u32[]{:S(2)}) collective-permute-start(bf16[32,16,128]{2,1,0:T(8,128)(2,1)} %get-tuple-element.19), channel_id=1, source_target_pairs={{0,96},{32,128},{64,160},{96,192},{128,224},{160,0},{192,32},{224,... | collective-permute-start | bytes 393224 | tf_op jit(solution)/shard_map/ppermute | solution.py:289
  51.3 18.0 %collective-permute-start.10 = (bf16[32,16,128]{2,1,0:T(8,128)(2,1)}, bf16[32,16,128]{2,1,0:T(8,128)(2,1)S(1)}, u32[]{:S(2)}, u32[]{:S(2)}) collective-permute-start(bf16[32,16,128]{2,1,0:T(8,128)(2,1)} %get-tuple-element.20), channel_id=1, source_target_pairs={{0,128},{32,160},{64,192},{96,224},{128,0},{160,32},{192,64},{224,... | collective-permute-start | bytes 393224 | tf_op jit(solution)/shard_map/ppermute | solution.py:289
  51.8 20.7 %collective-permute-start.11 = (bf16[32,16,128]{2,1,0:T(8,128)(2,1)}, bf16[32,16,128]{2,1,0:T(8,128)(2,1)S(1)}, u32[]{:S(2)}, u32[]{:S(2)}) collective-permute-start(bf16[32,16,128]{2,1,0:T(8,128)(2,1)} %get-tuple-element.21), channel_id=1, source_target_pairs={{0,160},{32,192},{64,224},{96,0},{128,32},{160,64},{192,96},{224,1... | collective-permute-start | bytes 393224 | tf_op jit(solution)/shard_map/ppermute | solution.py:289
  56.8 19.1 %collective-permute-start.12 = (bf16[32,16,128]{2,1,0:T(8,128)(2,1)}, bf16[32,16,128]{2,1,0:T(8,128)(2,1)S(1)}, u32[]{:S(2)}, u32[]{:S(2)}) collective-permute-start(bf16[32,16,128]{2,1,0:T(8,128)(2,1)} %get-tuple-element.22), channel_id=1, source_target_pairs={{0,192},{32,224},{64,0},{96,32},{128,64},{160,96},{192,128},{224,1... | collective-permute-start | bytes 393224 | tf_op jit(solution)/shard_map/ppermute | solution.py:289
  60.5 16.0 %collective-permute-start.13 = (bf16[32,16,128]{2,1,0:T(8,128)(2,1)}, bf16[32,16,128]{2,1,0:T(8,128)(2,1)S(1)}, u32[]{:S(2)}, u32[]{:S(2)}) collective-permute-start(bf16[32,16,128]{2,1,0:T(8,128)(2,1)} %get-tuple-element.23), channel_id=1, source_target_pairs={{0,224},{32,0},{64,32},{96,64},{128,96},{160,128},{192,160},{224,1... | collective-permute-start | bytes 393224 | tf_op jit(solution)/shard_map/ppermute | solution.py:289
  76.6 0.9 copy-start.16
  78.6 62.4 %all-to-all-start.1 = ((bf16[32,8,16,128]{3,2,1,0:T(8,128)(2,1)}), bf16[32,8,16,128]{3,2,1,0:T(8,128)(2,1)}, u32[]{:S(2)}, u32[]{:S(2)}) async-start(bf16[32,8,16,128]{3,2,1,0:T(8,128)(2,1)} %stack.1), calls=%async_computation.1 | async-start | bytes 2097152 | tf_op jit(solution)/shard_map/all_to_all | solution.py:298
  86.2 13.2 %collective-permute-start.20 = (bf16[32,16,128]{2,1,0:T(8,128)(2,1)S(1)}, bf16[32,16,128]{2,1,0:T(8,128)(2,1)S(1)}, u32[]{:S(2)}, u32[]{:S(2)}) collective-permute-start(bf16[32,16,128]{2,1,0:T(8,128)(2,1)S(1)} %get-tuple-element.25), channel_id=1, source_target_pairs={{0,224},{32,0},{64,32},{96,64},{128,96},{160,128},{192,160},{224,1... | collective-permute-start | bytes 393224 | tf_op jit(solution)/shard_map/ppermute | solution.py:289
  89.0 16.5 %collective-permute-start.19 = (bf16[32,16,128]{2,1,0:T(8,128)(2,1)S(1)}, bf16[32,16,128]{2,1,0:T(8,128)(2,1)S(1)}, u32[]{:S(2)}, u32[]{:S(2)}) collective-permute-start(bf16[32,16,128]{2,1,0:T(8,128)(2,1)S(1)} %get-tuple-element.26), channel_id=1, source_target_pairs={{0,192},{32,224},{64,0},{96,32},{128,64},{160,96},{192,128},{224,1... | collective-permute-start | bytes 393224 | tf_op jit(solution)/shard_map/ppermute | solution.py:289
  89.9 16.6 %collective-permute-start.18 = (bf16[32,16,128]{2,1,0:T(8,128)(2,1)S(1)}, bf16[32,16,128]{2,1,0:T(8,128)(2,1)S(1)}, u32[]{:S(2)}, u32[]{:S(2)}) collective-permute-start(bf16[32,16,128]{2,1,0:T(8,128)(2,1)S(1)} %get-tuple-element.27), channel_id=1, source_target_pairs={{0,160},{32,192},{64,224},{96,0},{128,32},{160,64},{192,96},{224,1... | collective-permute-start | bytes 393224 | tf_op jit(solution)/shard_map/ppermute | solution.py:289
  93.8 20.3 %collective-permute-start.17 = (bf16[32,16,128]{2,1,0:T(8,128)(2,1)S(1)}, bf16[32,16,128]{2,1,0:T(8,128)(2,1)S(1)}, u32[]{:S(2)}, u32[]{:S(2)}) collective-permute-start(bf16[32,16,128]{2,1,0:T(8,128)(2,1)S(1)} %get-tuple-element.28), channel_id=1, source_target_pairs={{0,128},{32,160},{64,192},{96,224},{128,0},{160,32},{192,64},{224,... | collective-permute-start | bytes 393224 | tf_op jit(solution)/shard_map/ppermute | solution.py:289
  95.0 20.8 %collective-permute-start.16 = (bf16[32,16,128]{2,1,0:T(8,128)(2,1)S(1)}, bf16[32,16,128]{2,1,0:T(8,128)(2,1)S(1)}, u32[]{:S(2)}, u32[]{:S(2)}) collective-permute-start(bf16[32,16,128]{2,1,0:T(8,128)(2,1)S(1)} %get-tuple-element.29), channel_id=1, source_target_pairs={{0,96},{32,128},{64,160},{96,192},{128,224},{160,0},{192,32},{224,... | collective-permute-start | bytes 393224 | tf_op jit(solution)/shard_map/ppermute | solution.py:289
  99.4 20.1 %collective-permute-start.15 = (bf16[32,16,128]{2,1,0:T(8,128)(2,1)S(1)}, bf16[32,16,128]{2,1,0:T(8,128)(2,1)S(1)}, u32[]{:S(2)}, u32[]{:S(2)}) collective-permute-start(bf16[32,16,128]{2,1,0:T(8,128)(2,1)S(1)} %get-tuple-element.30), channel_id=1, source_target_pairs={{0,64},{32,96},{64,128},{96,160},{128,192},{160,224},{192,0},{224,... | collective-permute-start | bytes 393224 | tf_op jit(solution)/shard_map/ppermute | solution.py:289
  105.5 0.6 copy-start
  106.1 18.6 %collective-permute-start.14 = (bf16[32,16,128]{2,1,0:T(8,128)(2,1)S(1)}, bf16[32,16,128]{2,1,0:T(8,128)(2,1)S(1)}, u32[]{:S(2)}, u32[]{:S(2)}) collective-permute-start(bf16[32,16,128]{2,1,0:T(8,128)(2,1)S(1)} %get-tuple-element.31), channel_id=1, source_target_pairs={{0,32},{32,64},{64,96},{96,128},{128,160},{160,192},{192,224},{224... | collective-permute-start | bytes 393224 | tf_op jit(solution)/shard_map/ppermute | solution.py:289
  106.5 0.7 copy-start.2
  107.2 22.0 %collective-permute-start.6 = (bf16[32,16,128]{2,1,0:T(8,128)(2,1)S(1)}, bf16[32,16,128]{2,1,0:T(8,128)(2,1)S(1)}, u32[]{:S(2)}, u32[]{:S(2)}) collective-permute-start(bf16[32,16,128]{2,1,0:T(8,128)(2,1)S(1)} %get-tuple-element.33), channel_id=1, source_target_pairs={{0,224},{32,0},{64,32},{96,64},{128,96},{160,128},{192,160},{224,1... | collective-permute-start | bytes 393224 | tf_op jit(solution)/shard_map/ppermute | solution.py:289
  114.0 0.6 copy-start.4
  114.7 21.7 %collective-permute-start.5 = (bf16[32,16,128]{2,1,0:T(8,128)(2,1)S(1)}, bf16[32,16,128]{2,1,0:T(8,128)(2,1)S(1)}, u32[]{:S(2)}, u32[]{:S(2)}) collective-permute-start(bf16[32,16,128]{2,1,0:T(8,128)(2,1)S(1)} %get-tuple-element.34), channel_id=1, source_target_pairs={{0,192},{32,224},{64,0},{96,32},{128,64},{160,96},{192,128},{224,1... | collective-permute-start | bytes 393224 | tf_op jit(solution)/shard_map/ppermute | solution.py:289
  115.8 0.6 copy-start.6
  116.5 37.0 %collective-permute-start.4 = (bf16[32,16,128]{2,1,0:T(8,128)(2,1)}, bf16[32,16,128]{2,1,0:T(8,128)(2,1)}, u32[]{:S(2)}, u32[]{:S(2)}) collective-permute-start(bf16[32,16,128]{2,1,0:T(8,128)(2,1)} %get-tuple-element.35), channel_id=1, source_target_pairs={{0,160},{32,192},{64,224},{96,0},{128,32},{160,64},{192,96},{224,1... | collective-permute-start | bytes 393224 | tf_op jit(solution)/shard_map/ppermute | solution.py:289
  119.5 0.7 copy-start.12
  120.1 33.3 %collective-permute-start.3 = (bf16[32,16,128]{2,1,0:T(8,128)(2,1)}, bf16[32,16,128]{2,1,0:T(8,128)(2,1)}, u32[]{:S(2)}, u32[]{:S(2)}) collective-permute-start(bf16[32,16,128]{2,1,0:T(8,128)(2,1)} %get-tuple-element.36), channel_id=1, source_target_pairs={{0,128},{32,160},{64,192},{96,224},{128,0},{160,32},{192,64},{224,... | collective-permute-start | bytes 393224 | tf_op jit(solution)/shard_map/ppermute | solution.py:289
  124.7 0.7 copy-start.14
  125.4 28.1 %collective-permute-start.2 = (bf16[32,16,128]{2,1,0:T(8,128)(2,1)}, bf16[32,16,128]{2,1,0:T(8,128)(2,1)}, u32[]{:S(2)}, u32[]{:S(2)}) collective-permute-start(bf16[32,16,128]{2,1,0:T(8,128)(2,1)} %get-tuple-element.37), channel_id=1, source_target_pairs={{0,96},{32,128},{64,160},{96,192},{128,224},{160,0},{192,32},{224,... | collective-permute-start | bytes 393224 | tf_op jit(solution)/shard_map/ppermute | solution.py:289
  129.2 0.7 copy-start.8
  129.9 23.6 %collective-permute-start.1 = (bf16[32,16,128]{2,1,0:T(8,128)(2,1)}, bf16[32,16,128]{2,1,0:T(8,128)(2,1)}, u32[]{:S(2)}, u32[]{:S(2)}) collective-permute-start(bf16[32,16,128]{2,1,0:T(8,128)(2,1)} %get-tuple-element.38), channel_id=1, source_target_pairs={{0,64},{32,96},{64,128},{96,160},{128,192},{160,224},{192,0},{224,... | collective-permute-start | bytes 393224 | tf_op jit(solution)/shard_map/ppermute | solution.py:289
  136.4 0.6 copy-start.10
  137.0 16.4 %collective-permute-start = (bf16[32,16,128]{2,1,0:T(8,128)(2,1)}, bf16[32,16,128]{2,1,0:T(8,128)(2,1)}, u32[]{:S(2)}, u32[]{:S(2)}) collective-permute-start(bf16[32,16,128]{2,1,0:T(8,128)(2,1)} %get-tuple-element.39), channel_id=1, source_target_pairs={{0,32},{32,64},{64,96},{96,128},{128,160},{160,192},{192,224},{224... | collective-permute-start | bytes 393224 | tf_op jit(solution)/shard_map/ppermute | solution.py:289
  141.0 0.9 copy-start.1
  141.9 0.9 copy-start.3
  142.8 0.9 copy-start.5
  143.7 0.9 copy-start.7
  144.6 0.9 copy-start.13
  145.5 0.9 copy-start.15
  146.4 7.0 %copy-start.9 = (bf16[32,16,128]{2,1,0:T(8,128)(2,1)S(1)}, bf16[32,16,128]{2,1,0:T(8,128)(2,1)}, u32[]{:S(2)}) copy-start(bf16[32,16,128]{2,1,0:T(8,128)(2,1)} %copy-done.8) | copy-start | bytes 393220
  146.4 7.0 %copy-start.11 = (bf16[32,16,128]{2,1,0:T(8,128)(2,1)S(1)}, bf16[32,16,128]{2,1,0:T(8,128)(2,1)}, u32[]{:S(2)}) copy-start(bf16[32,16,128]{2,1,0:T(8,128)(2,1)} %copy-done.10) | copy-start | bytes 393220

commit v4 on v3

--- a/solution.py
+++ b/solution.py
@@ -150,7 +150,7 @@
             pltpu.VMEM((slots, 256, waves), F32),
             pltpu.VMEM((512, 512), BF16),
             pltpu.VMEM((lats, lats), BF16),
-            pltpu.VMEM((8, slots * PITCH, 128), F32),
+            pltpu.VMEM((8, (slots + 1) * PITCH, 128), F32),
             *[pltpu.VMEM(out, BF16) for out in outs],
             pltpu.SemaphoreType.DMA((members,)),
             pltpu.SemaphoreType.DMA((slots,)),
@@ -167,19 +167,29 @@
 def basis_kernel(wave_ref, out_ref):
     lons = out_ref.shape[1]
     lanes = lax.broadcasted_iota(jnp.int32, (BAND, 128), 1).astype(F32)
-    step = 2.0 * math.pi / lons
-
-    def wrap(count, period):
-        return count - period * jnp.floor((count + 0.5) * (1.0 / period))
+
+    def turns(count, period):
+        return count - period * jnp.floor((count + 0.5) * (1.0 / period) + 0.5)
+
+    def circle(part):
+        half = part * math.pi
+        sq = half * half
+        sin_half = 0.0
+        for n in (13, 11, 9, 7, 5, 3, 1):
+            sin_half = sin_half * sq + (-1.0) ** (n // 2) / math.factorial(n)
+        sin_half = sin_half * half
+        cos_half = 0.0
+        for n in (12, 10, 8, 6, 4, 2, 0):
+            cos_half = cos_half * sq + (-1.0) ** (n // 2) / math.factorial(n)
+        return 1.0 - 2.0 * sin_half * sin_half, 2.0 * sin_half * cos_half
 
     def band(i, carry):
         wave = wave_ref[pl.ds(pl.multiple_of(i * BAND, BAND), BAND), :]
         count = wave * lanes
-        near = wrap(count, float(lons)) * step
-        far = wrap(count, lons / 128.0) * (128.0 * step)
+        near_cos, near_sin = circle(turns(count, float(lons)) * (1.0 / lons))
+        far_cos, far_sin = circle(turns(count, lons / 128.0) * (128.0 / lons))
         weight = jnp.where(wave == 0.0, 1.0, 2.0)
-        near_cos, near_sin = weight * jnp.cos(near), weight * jnp.sin(near)
-        far_cos, far_sin = jnp.cos(far), jnp.sin(far)
+        near_cos, near_sin = weight * near_cos, weight * near_sin
         for b in range(lons // 128):
             c, s = far_cos[:, b:b + 1], far_sin[:, b:b + 1]
             real = c * near_cos - s * near_sin

time: 159 us -> 158 us (level)
  no operation moved by 1% of the time
where the time goes in v4:
time: 158 us
  starting transfers between devices  68.9 us (44%)
  Pallas kernels  28.9 us (18%)
  waiting for transfers between devices  24.4 us (15%)
  blocking collectives  22.2 us (14%)
  local copies, waits for them, and re-layouts  12.9 us (8%)
    ppermute x21, starting transfers between devices, hop(): lax.ppermute(blocks[dz], 'z', [(i, (i + dz) % NZ) for i in range(NZ)])  54.9 us
    ppermute x21, waiting for transfers between devices, hop(): lax.ppermute(blocks[dz], 'z', [(i, (i + dz) % NZ) for i in range(NZ)])  24.4 us
    all_to_all x1, blocking collectives, plane(): return lax.all_to_all(block, ('y', 'c', 'mem'), 0, 0, tiled=True)  22.2 us
    all_to_all x2, starting transfers between devices, plane(): return lax.all_to_all(block, ('y', 'c', 'mem'), 0, 0, tiled=True)  14.1 us
    pallas_call x1, Pallas kernels, front(): pl.pallas_call(front_kernel, in_specs=[pl.BlockSpec(memory_space=pltpu.SM...  13.1 us
    pallas_call x2, Pallas kernels, back(): pl.pallas_call(functools.partial(back_kernel, counts=counts), grid=(lons...  11.9 us
    unnamed x36, local copies, waits for them, and re-layouts  11.5 us
  transfers between devices with their start and end apart: 23, of which 8 were waited for; matrix products, arithmetic and copies ran while one was open for 1% of the time, Pallas kernels for 7%

profile of v4, /device:TPU:2, one launch (start us, length us, event | category | flops | bytes accessed | tf_op | source)
XLA Modules:
  0.0 157.6 jit_solution(1400904943446315558)
XLA Ops:
  0.0 13.1 %front.1 = (bf16[32,16,128]{2,1,0:T(8,128)(2,1)}, bf16[32,16,128]{2,1,0:T(8,128)(2,1)}, bf16[32,16,128]{2,1,0:T(8,128)(2,1)}, bf16[32,16,128]{2,1,0:T(8,128)(2,1...) custom-call(s32[1]{0:T(128)} %bitcast.z_ref, ...), custom_call_target="tpu_custom_call" | custom-call | tf_op jit(solution)/shard_map/front/pallas_call | solution.py:142
  13.1 22.2 %all_to_all.15 = bf16[32,8,16,128]{3,2,1,0:T(8,128)(2,1)S(1)} all-to-all(bf16[32,8,16,128]{3,2,1,0:T(8,128)(2,1)} %get-tuple-element.15), channel_id=1, replica_groups=mesh['z'=8,'y'=4,'c'=2,'mem'=4] {'y','c','mem'}, dimensions={0} | all-to-all | bytes 2097152 | tf_op jit(solution)/shard_map/all_to_all | solution.py:308
  35.3 6.6 %all-to-all-start.2 = ((bf16[32,8,16,128]{3,2,1,0:T(8,128)(2,1)}), bf16[32,8,16,128]{3,2,1,0:T(8,128)(2,1)S(1)}, u32[]{:S(2)}, u32[]{:S(2)}) async-start(bf16[32,8,16,128]{3,2,1,0:T(8,128)(2,1)} %get-tuple-element.24), calls=%async_computation.2 | async-start | bytes 2097152 | tf_op jit(solution)/shard_map/all_to_all | solution.py:308
  42.0 2.0 %collective-permute-start.7 = (bf16[32,16,128]{2,1,0:T(8,128)(2,1)}, bf16[32,16,128]{2,1,0:T(8,128)(2,1)S(1)}, u32[]{:S(2)}, u32[]{:S(2)}) collective-permute-start(bf16[32,16,128]{2,1,0:T(8,128)(2,1)} %get-tuple-element.17), channel_id=1, source_target_pairs={{0,32},{32,64},{64,96},{96,128},{128,160},{160,192},{192,224},{224... | collective-permute-start | bytes 393224 | tf_op jit(solution)/shard_map/ppermute | solution.py:299
  44.0 3.3 %collective-permute-start.8 = (bf16[32,16,128]{2,1,0:T(8,128)(2,1)}, bf16[32,16,128]{2,1,0:T(8,128)(2,1)S(1)}, u32[]{:S(2)}, u32[]{:S(2)}) collective-permute-start(bf16[32,16,128]{2,1,0:T(8,128)(2,1)} %get-tuple-element.18), channel_id=1, source_target_pairs={{0,64},{32,96},{64,128},{96,160},{128,192},{160,224},{192,0},{224,... | collective-permute-start | bytes 393224 | tf_op jit(solution)/shard_map/ppermute | solution.py:299
  47.2 4.0 %collective-permute-start.9 = (bf16[32,16,128]{2,1,0:T(8,128)(2,1)}, bf16[32,16,128]{2,1,0:T(8,128)(2,1)S(1)}, u32[]{:S(2)}, u32[]{:S(2)}) collective-permute-start(bf16[32,16,128]{2,1,0:T(8,128)(2,1)} %get-tuple-element.19), channel_id=1, source_target_pairs={{0,96},{32,128},{64,160},{96,192},{128,224},{160,0},{192,32},{224,... | collective-permute-start | bytes 393224 | tf_op jit(solution)/shard_map/ppermute | solution.py:299
  51.8 4.9 %collective-permute-start.11 = (bf16[32,16,128]{2,1,0:T(8,128)(2,1)}, bf16[32,16,128]{2,1,0:T(8,128)(2,1)S(1)}, u32[]{:S(2)}, u32[]{:S(2)}) collective-permute-start(bf16[32,16,128]{2,1,0:T(8,128)(2,1)} %get-tuple-element.21), channel_id=1, source_target_pairs={{0,160},{32,192},{64,224},{96,0},{128,32},{160,64},{192,96},{224,1... | collective-permute-start | bytes 393224 | tf_op jit(solution)/shard_map/ppermute | solution.py:299
  56.8 2.7 %collective-permute-start.12 = (bf16[32,16,128]{2,1,0:T(8,128)(2,1)}, bf16[32,16,128]{2,1,0:T(8,128)(2,1)S(1)}, u32[]{:S(2)}, u32[]{:S(2)}) collective-permute-start(bf16[32,16,128]{2,1,0:T(8,128)(2,1)} %get-tuple-element.22), channel_id=1, source_target_pairs={{0,192},{32,224},{64,0},{96,32},{128,64},{160,96},{192,128},{224,1... | collective-permute-start | bytes 393224 | tf_op jit(solution)/shard_map/ppermute | solution.py:299
  59.4 1.1 collective-permute-done.8.refs_2_
  60.5 3.3 %collective-permute-start.13 = (bf16[32,16,128]{2,1,0:T(8,128)(2,1)}, bf16[32,16,128]{2,1,0:T(8,128)(2,1)S(1)}, u32[]{:S(2)}, u32[]{:S(2)}) collective-permute-start(bf16[32,16,128]{2,1,0:T(8,128)(2,1)} %get-tuple-element.23), channel_id=1, source_target_pairs={{0,224},{32,0},{64,32},{96,64},{128,96},{160,128},{192,160},{224,1... | collective-permute-start | bytes 393224 | tf_op jit(solution)/shard_map/ppermute | solution.py:299
  63.9 5.4 %collective-permute-done.9.refs_3_ = bf16[32,16,128]{2,1,0:T(8,128)(2,1)S(1)} collective-permute-done((bf16[32,16,128]{2,1,0:T(8,128)(2,1)}, bf16[32,16,128]{2,1,0:T(8,128)(2,1)S(1)}, u32[]{:S(2)}, u32[]{:S(2)}) %collective-permute-start.9) | collective-permute-done | bytes 131104 | tf_op jit(solution)/shard_map/ppermute | solution.py:299
  69.3 3.3 %collective-permute-done.11.refs_5_ = bf16[32,16,128]{2,1,0:T(8,128)(2,1)S(1)} collective-permute-done((bf16[32,16,128]{2,1,0:T(8,128)(2,1)}, bf16[32,16,128]{2,1,0:T(8,128)(2,1)S(1)}, u32[]{:S(2)}, u32[]{:S(2)}) %collective-permute-start.11) | collective-permute-done | bytes 131104 | tf_op jit(solution)/shard_map/ppermute | solution.py:299
  72.5 3.4 %collective-permute-done.12.refs_6_ = bf16[32,16,128]{2,1,0:T(8,128)(2,1)S(1)} collective-permute-done((bf16[32,16,128]{2,1,0:T(8,128)(2,1)}, bf16[32,16,128]{2,1,0:T(8,128)(2,1)S(1)}, u32[]{:S(2)}, u32[]{:S(2)}) %collective-permute-start.12) | collective-permute-done | bytes 131104 | tf_op jit(solution)/shard_map/ppermute | solution.py:299
  75.9 0.7 collective-permute-done.13.refs_7_
  76.6 0.9 copy-done.16
  77.5 1.1 stack.1
  78.6 7.4 %all-to-all-start.1 = ((bf16[32,8,16,128]{3,2,1,0:T(8,128)(2,1)}), bf16[32,8,16,128]{3,2,1,0:T(8,128)(2,1)}, u32[]{:S(2)}, u32[]{:S(2)}) async-start(bf16[32,8,16,128]{3,2,1,0:T(8,128)(2,1)} %stack.1), calls=%async_computation.1 | async-start | bytes 2097152 | tf_op jit(solution)/shard_map/all_to_all | solution.py:308
  86.2 2.7 %collective-permute-start.20 = (bf16[32,16,128]{2,1,0:T(8,128)(2,1)S(1)}, bf16[32,16,128]{2,1,0:T(8,128)(2,1)S(1)}, u32[]{:S(2)}, u32[]{:S(2)}) collective-permute-start(bf16[32,16,128]{2,1,0:T(8,128)(2,1)S(1)} %get-tuple-element.25), channel_id=1, source_target_pairs={{0,224},{32,0},{64,32},{96,64},{128,96},{160,128},{192,160},{224,1... | collective-permute-start | bytes 393224 | tf_op jit(solution)/shard_map/ppermute | solution.py:299
  89.0 0.9 collective-permute-start.19
  89.9 3.8 %collective-permute-start.18 = (bf16[32,16,128]{2,1,0:T(8,128)(2,1)S(1)}, bf16[32,16,128]{2,1,0:T(8,128)(2,1)S(1)}, u32[]{:S(2)}, u32[]{:S(2)}) collective-permute-start(bf16[32,16,128]{2,1,0:T(8,128)(2,1)S(1)} %get-tuple-element.27), channel_id=1, source_target_pairs={{0,160},{32,192},{64,224},{96,0},{128,32},{160,64},{192,96},{224,1... | collective-permute-start | bytes 393224 | tf_op jit(solution)/shard_map/ppermute | solution.py:299
  93.7 1.2 collective-permute-start.17
  95.0 3.5 %collective-permute-start.16 = (bf16[32,16,128]{2,1,0:T(8,128)(2,1)S(1)}, bf16[32,16,128]{2,1,0:T(8,128)(2,1)S(1)}, u32[]{:S(2)}, u32[]{:S(2)}) collective-permute-start(bf16[32,16,128]{2,1,0:T(8,128)(2,1)S(1)} %get-tuple-element.29), channel_id=1, source_target_pairs={{0,96},{32,128},{64,160},{96,192},{128,224},{160,0},{192,32},{224,... | collective-permute-start | bytes 393224 | tf_op jit(solution)/shard_map/ppermute | solution.py:299
  98.5 0.9 slice_bitcast_fusion.7
  99.4 2.4 %collective-permute-start.15 = (bf16[32,16,128]{2,1,0:T(8,128)(2,1)S(1)}, bf16[32,16,128]{2,1,0:T(8,128)(2,1)S(1)}, u32[]{:S(2)}, u32[]{:S(2)}) collective-permute-start(bf16[32,16,128]{2,1,0:T(8,128)(2,1)S(1)} %get-tuple-element.30), channel_id=1, source_target_pairs={{0,64},{32,96},{64,128},{96,160},{128,192},{160,224},{192,0},{224,... | collective-permute-start | bytes 393224 | tf_op jit(solution)/shard_map/ppermute | solution.py:299
  101.8 3.7 %collective-permute-done.19 = bf16[32,16,128]{2,1,0:T(8,128)(2,1)S(1)} collective-permute-done((bf16[32,16,128]{2,1,0:T(8,128)(2,1)S(1)}, bf16[32,16,128]{2,1,0:T(8,128)(2,1)S(1)}, u32[]{:S(2)}, u32[]{:S(2)}) %collective-permute-start.19) | collective-permute-done | bytes 131104 | tf_op jit(solution)/shard_map/ppermute | solution.py:299
  105.5 0.6 copy-done
  106.5 0.7 copy-done.2
  107.2 6.9 %collective-permute-start.6 = (bf16[32,16,128]{2,1,0:T(8,128)(2,1)S(1)}, bf16[32,16,128]{2,1,0:T(8,128)(2,1)S(1)}, u32[]{:S(2)}, u32[]{:S(2)}) collective-permute-start(bf16[32,16,128]{2,1,0:T(8,128)(2,1)S(1)} %get-tuple-element.33), channel_id=1, source_target_pairs={{0,224},{32,0},{64,32},{96,64},{128,96},{160,128},{192,160},{224,1... | collective-permute-start | bytes 393224 | tf_op jit(solution)/shard_map/ppermute | solution.py:299
  114.0 0.6 copy-done.4
  114.7 1.1 collective-permute-start.5
  115.8 0.6 copy-done.6
  116.5 3.0 %collective-permute-start.4 = (bf16[32,16,128]{2,1,0:T(8,128)(2,1)}, bf16[32,16,128]{2,1,0:T(8,128)(2,1)}, u32[]{:S(2)}, u32[]{:S(2)}) collective-permute-start(bf16[32,16,128]{2,1,0:T(8,128)(2,1)} %get-tuple-element.35), channel_id=1, source_target_pairs={{0,160},{32,192},{64,224},{96,0},{128,32},{160,64},{192,96},{224,1... | collective-permute-start | bytes 393224 | tf_op jit(solution)/shard_map/ppermute | solution.py:299
  119.5 0.6 copy-done.12
  120.1 4.6 %collective-permute-start.3 = (bf16[32,16,128]{2,1,0:T(8,128)(2,1)}, bf16[32,16,128]{2,1,0:T(8,128)(2,1)}, u32[]{:S(2)}, u32[]{:S(2)}) collective-permute-start(bf16[32,16,128]{2,1,0:T(8,128)(2,1)} %get-tuple-element.36), channel_id=1, source_target_pairs={{0,128},{32,160},{64,192},{96,224},{128,0},{160,32},{192,64},{224,... | collective-permute-start | bytes 393224 | tf_op jit(solution)/shard_map/ppermute | solution.py:299
  124.7 0.7 copy-done.14
  125.4 3.8 %collective-permute-start.2 = (bf16[32,16,128]{2,1,0:T(8,128)(2,1)}, bf16[32,16,128]{2,1,0:T(8,128)(2,1)}, u32[]{:S(2)}, u32[]{:S(2)}) collective-permute-start(bf16[32,16,128]{2,1,0:T(8,128)(2,1)} %get-tuple-element.37), channel_id=1, source_target_pairs={{0,96},{32,128},{64,160},{96,192},{128,224},{160,0},{192,32},{224,... | collective-permute-start | bytes 393224 | tf_op jit(solution)/shard_map/ppermute | solution.py:299
  129.2 0.7 copy-done.8
  129.9 6.5 %collective-permute-done.5 = bf16[32,16,128]{2,1,0:T(8,128)(2,1)S(1)} collective-permute-done((bf16[32,16,128]{2,1,0:T(8,128)(2,1)S(1)}, bf16[32,16,128]{2,1,0:T(8,128)(2,1)S(1)}, u32[]{:S(2)}, u32[]{:S(2)}) %collective-permute-start.5) | collective-permute-done | bytes 131104 | tf_op jit(solution)/shard_map/ppermute | solution.py:299
  136.4 0.6 copy-done.10
  137.3 2.8 %basis.1.refs_9_.refs_8_ = bf16[1024,1536]{1,0:T(8,128)(2,1)S(1)} custom-call(f32[512,128]{1,0:T(8,128)S(1)} %broadcast_in_dim.2.wave_ref), custom_call_target="tpu_custom_call" | custom-call | tf_op jit(solution)/shard_map/basis/pallas_call | solution.py:208
  140.2 0.9 copy-done.1
  141.1 0.9 copy-done.3
  142.0 0.9 copy-done.5
  142.9 0.9 copy-done.7
  143.8 0.9 copy-done.13
  144.7 0.9 copy-done.15
  145.6 7.0 %back.2.refs_10_ = bf16[12,8,1536]{2,1,0:T(8,128)(2,1)} custom-call(bf16[8,4,8,16,128]{4,3,2,1,0:T(8,128)(2,1)} %bitcast.18.refs_0_, bf16[8,4,16,128]{3,2,1,0:T(8,128)(2,1)S(1)} %bitcast.48, bf16[8,4,16,128]{3,2,1,0:T(8,128)(2,1)S(1)} %bitcast.58, bf16[8,4,16,128]{3,2,1,0:T(8,128)(2,1)S(1)} %bitcast.57, bf16[8,4,16,128]{3,2,1,0:T(8,128)(2,1)S(1)} %bitcast.54, ...), custom_call_target="tpu_custom_call" | custom-call | tf_op jit(solution)/shard_map/back/pallas_call | solution.py:283
  152.7 4.9 %back.3 = bf16[12,8,1536]{2,1,0:T(8,128)(2,1)} custom-call(bf16[8,4,16,128]{3,2,1,0:T(8,128)(2,1)S(1)} %bitcast.49, bf16[8,4,16,128]{3,2,1,0:T(8,128)(2,1)} %bitcast.5.refs_1_, bf16[8,4,16,128]{3,2,1,0:T(8,128)(2,1)} %bitcast.7.refs_2_, bf16[8,4,16,128]{3,2,1,0:T(8,128)(2,1)} %bitcast.9.refs_3_, ...), custom_call_target="tpu_custom_call", output_to_operand_aliasing={{}: (10, {})} | custom-call | tf_op jit(solution)/shard_map/back/pallas_call | solution.py:283
  (47 shorter events, 1.5 us)
Async XLA Ops:
  35.3 43.3 %all-to-all-start.2 = ((bf16[32,8,16,128]{3,2,1,0:T(8,128)(2,1)}), bf16[32,8,16,128]{3,2,1,0:T(8,128)(2,1)S(1)}, u32[]{:S(2)}, u32[]{:S(2)}) async-start(bf16[32,8,16,128]{3,2,1,0:T(8,128)(2,1)} %get-tuple-element.24), calls=%async_computation.2 | async-start | bytes 2097152 | tf_op jit(solution)/shard_map/all_to_all | solution.py:308
  42.0 95.1 %copy-start.17 = (s32[512]{0:T(512)S(1)}, s32[512]{0:T(512)}, u32[]{:S(2)}) copy-start(s32[512]{0:T(512)} %param.11) | copy-start | bytes 6148
  42.0 14.8 %collective-permute-start.7 = (bf16[32,16,128]{2,1,0:T(8,128)(2,1)}, bf16[32,16,128]{2,1,0:T(8,128)(2,1)S(1)}, u32[]{:S(2)}, u32[]{:S(2)}) collective-permute-start(bf16[32,16,128]{2,1,0:T(8,128)(2,1)} %get-tuple-element.17), channel_id=1, source_target_pairs={{0,32},{32,64},{64,96},{96,128},{128,160},{160,192},{192,224},{224... | collective-permute-start | bytes 393224 | tf_op jit(solution)/shard_map/ppermute | solution.py:299
  44.0 16.6 %collective-permute-start.8 = (bf16[32,16,128]{2,1,0:T(8,128)(2,1)}, bf16[32,16,128]{2,1,0:T(8,128)(2,1)S(1)}, u32[]{:S(2)}, u32[]{:S(2)}) collective-permute-start(bf16[32,16,128]{2,1,0:T(8,128)(2,1)} %get-tuple-element.18), channel_id=1, source_target_pairs={{0,64},{32,96},{64,128},{96,160},{128,192},{160,224},{192,0},{224,... | collective-permute-start | bytes 393224 | tf_op jit(solution)/shard_map/ppermute | solution.py:299
  47.2 22.0 %collective-permute-start.9 = (bf16[32,16,128]{2,1,0:T(8,128)(2,1)}, bf16[32,16,128]{2,1,0:T(8,128)(2,1)S(1)}, u32[]{:S(2)}, u32[]{:S(2)}) collective-permute-start(bf16[32,16,128]{2,1,0:T(8,128)(2,1)} %get-tuple-element.19), channel_id=1, source_target_pairs={{0,96},{32,128},{64,160},{96,192},{128,224},{160,0},{192,32},{224,... | collective-permute-start | bytes 393224 | tf_op jit(solution)/shard_map/ppermute | solution.py:299
  51.3 18.0 %collective-permute-start.10 = (bf16[32,16,128]{2,1,0:T(8,128)(2,1)}, bf16[32,16,128]{2,1,0:T(8,128)(2,1)S(1)}, u32[]{:S(2)}, u32[]{:S(2)}) collective-permute-start(bf16[32,16,128]{2,1,0:T(8,128)(2,1)} %get-tuple-element.20), channel_id=1, source_target_pairs={{0,128},{32,160},{64,192},{96,224},{128,0},{160,32},{192,64},{224,... | collective-permute-start | bytes 393224 | tf_op jit(solution)/shard_map/ppermute | solution.py:299
  51.8 20.7 %collective-permute-start.11 = (bf16[32,16,128]{2,1,0:T(8,128)(2,1)}, bf16[32,16,128]{2,1,0:T(8,128)(2,1)S(1)}, u32[]{:S(2)}, u32[]{:S(2)}) collective-permute-start(bf16[32,16,128]{2,1,0:T(8,128)(2,1)} %get-tuple-element.21), channel_id=1, source_target_pairs={{0,160},{32,192},{64,224},{96,0},{128,32},{160,64},{192,96},{224,1... | collective-permute-start | bytes 393224 | tf_op jit(solution)/shard_map/ppermute | solution.py:299
  56.8 19.1 %collective-permute-start.12 = (bf16[32,16,128]{2,1,0:T(8,128)(2,1)}, bf16[32,16,128]{2,1,0:T(8,128)(2,1)S(1)}, u32[]{:S(2)}, u32[]{:S(2)}) collective-permute-start(bf16[32,16,128]{2,1,0:T(8,128)(2,1)} %get-tuple-element.22), channel_id=1, source_target_pairs={{0,192},{32,224},{64,0},{96,32},{128,64},{160,96},{192,128},{224,1... | collective-permute-start | bytes 393224 | tf_op jit(solution)/shard_map/ppermute | solution.py:299
  60.5 16.0 %collective-permute-start.13 = (bf16[32,16,128]{2,1,0:T(8,128)(2,1)}, bf16[32,16,128]{2,1,0:T(8,128)(2,1)S(1)}, u32[]{:S(2)}, u32[]{:S(2)}) collective-permute-start(bf16[32,16,128]{2,1,0:T(8,128)(2,1)} %get-tuple-element.23), channel_id=1, source_target_pairs={{0,224},{32,0},{64,32},{96,64},{128,96},{160,128},{192,160},{224,1... | collective-permute-start | bytes 393224 | tf_op jit(solution)/shard_map/ppermute | solution.py:299
  76.6 0.9 copy-start.16
  78.6 61.6 %all-to-all-start.1 = ((bf16[32,8,16,128]{3,2,1,0:T(8,128)(2,1)}), bf16[32,8,16,128]{3,2,1,0:T(8,128)(2,1)}, u32[]{:S(2)}, u32[]{:S(2)}) async-start(bf16[32,8,16,128]{3,2,1,0:T(8,128)(2,1)} %stack.1), calls=%async_computation.1 | async-start | bytes 2097152 | tf_op jit(solution)/shard_map/all_to_all | solution.py:308
  86.2 13.2 %collective-permute-start.20 = (bf16[32,16,128]{2,1,0:T(8,128)(2,1)S(1)}, bf16[32,16,128]{2,1,0:T(8,128)(2,1)S(1)}, u32[]{:S(2)}, u32[]{:S(2)}) collective-permute-start(bf16[32,16,128]{2,1,0:T(8,128)(2,1)S(1)} %get-tuple-element.25), channel_id=1, source_target_pairs={{0,224},{32,0},{64,32},{96,64},{128,96},{160,128},{192,160},{224,1... | collective-permute-start | bytes 393224 | tf_op jit(solution)/shard_map/ppermute | solution.py:299
  89.0 16.5 %collective-permute-start.19 = (bf16[32,16,128]{2,1,0:T(8,128)(2,1)S(1)}, bf16[32,16,128]{2,1,0:T(8,128)(2,1)S(1)}, u32[]{:S(2)}, u32[]{:S(2)}) collective-permute-start(bf16[32,16,128]{2,1,0:T(8,128)(2,1)S(1)} %get-tuple-element.26), channel_id=1, source_target_pairs={{0,192},{32,224},{64,0},{96,32},{128,64},{160,96},{192,128},{224,1... | collective-permute-start | bytes 393224 | tf_op jit(solution)/shard_map/ppermute | solution.py:299
  89.9 16.6 %collective-permute-start.18 = (bf16[32,16,128]{2,1,0:T(8,128)(2,1)S(1)}, bf16[32,16,128]{2,1,0:T(8,128)(2,1)S(1)}, u32[]{:S(2)}, u32[]{:S(2)}) collective-permute-start(bf16[32,16,128]{2,1,0:T(8,128)(2,1)S(1)} %get-tuple-element.27), channel_id=1, source_target_pairs={{0,160},{32,192},{64,224},{96,0},{128,32},{160,64},{192,96},{224,1... | collective-permute-start | bytes 393224 | tf_op jit(solution)/shard_map/ppermute | solution.py:299
  93.7 20.3 %collective-permute-start.17 = (bf16[32,16,128]{2,1,0:T(8,128)(2,1)S(1)}, bf16[32,16,128]{2,1,0:T(8,128)(2,1)S(1)}, u32[]{:S(2)}, u32[]{:S(2)}) collective-permute-start(bf16[32,16,128]{2,1,0:T(8,128)(2,1)S(1)} %get-tuple-element.28), channel_id=1, source_target_pairs={{0,128},{32,160},{64,192},{96,224},{128,0},{160,32},{192,64},{224,... | collective-permute-start | bytes 393224 | tf_op jit(solution)/shard_map/ppermute | solution.py:299
  95.0 20.8 %collective-permute-start.16 = (bf16[32,16,128]{2,1,0:T(8,128)(2,1)S(1)}, bf16[32,16,128]{2,1,0:T(8,128)(2,1)S(1)}, u32[]{:S(2)}, u32[]{:S(2)}) collective-permute-start(bf16[32,16,128]{2,1,0:T(8,128)(2,1)S(1)} %get-tuple-element.29), channel_id=1, source_target_pairs={{0,96},{32,128},{64,160},{96,192},{128,224},{160,0},{192,32},{224,... | collective-permute-start | bytes 393224 | tf_op jit(solution)/shard_map/ppermute | solution.py:299
  99.4 20.1 %collective-permute-start.15 = (bf16[32,16,128]{2,1,0:T(8,128)(2,1)S(1)}, bf16[32,16,128]{2,1,0:T(8,128)(2,1)S(1)}, u32[]{:S(2)}, u32[]{:S(2)}) collective-permute-start(bf16[32,16,128]{2,1,0:T(8,128)(2,1)S(1)} %get-tuple-element.30), channel_id=1, source_target_pairs={{0,64},{32,96},{64,128},{96,160},{128,192},{160,224},{192,0},{224,... | collective-permute-start | bytes 393224 | tf_op jit(solution)/shard_map/ppermute | solution.py:299
  105.5 0.6 copy-start
  106.1 18.6 %collective-permute-start.14 = (bf16[32,16,128]{2,1,0:T(8,128)(2,1)S(1)}, bf16[32,16,128]{2,1,0:T(8,128)(2,1)S(1)}, u32[]{:S(2)}, u32[]{:S(2)}) collective-permute-start(bf16[32,16,128]{2,1,0:T(8,128)(2,1)S(1)} %get-tuple-element.31), channel_id=1, source_target_pairs={{0,32},{32,64},{64,96},{96,128},{128,160},{160,192},{192,224},{224... | collective-permute-start | bytes 393224 | tf_op jit(solution)/shard_map/ppermute | solution.py:299
  106.5 0.7 copy-start.2
  107.2 22.0 %collective-permute-start.6 = (bf16[32,16,128]{2,1,0:T(8,128)(2,1)S(1)}, bf16[32,16,128]{2,1,0:T(8,128)(2,1)S(1)}, u32[]{:S(2)}, u32[]{:S(2)}) collective-permute-start(bf16[32,16,128]{2,1,0:T(8,128)(2,1)S(1)} %get-tuple-element.33), channel_id=1, source_target_pairs={{0,224},{32,0},{64,32},{96,64},{128,96},{160,128},{192,160},{224,1... | collective-permute-start | bytes 393224 | tf_op jit(solution)/shard_map/ppermute | solution.py:299
  114.0 0.6 copy-start.4
  114.7 21.7 %collective-permute-start.5 = (bf16[32,16,128]{2,1,0:T(8,128)(2,1)S(1)}, bf16[32,16,128]{2,1,0:T(8,128)(2,1)S(1)}, u32[]{:S(2)}, u32[]{:S(2)}) collective-permute-start(bf16[32,16,128]{2,1,0:T(8,128)(2,1)S(1)} %get-tuple-element.34), channel_id=1, source_target_pairs={{0,192},{32,224},{64,0},{96,32},{128,64},{160,96},{192,128},{224,1... | collective-permute-start | bytes 393224 | tf_op jit(solution)/shard_map/ppermute | solution.py:299
  115.8 0.6 copy-start.6
  116.5 36.2 %collective-permute-start.4 = (bf16[32,16,128]{2,1,0:T(8,128)(2,1)}, bf16[32,16,128]{2,1,0:T(8,128)(2,1)}, u32[]{:S(2)}, u32[]{:S(2)}) collective-permute-start(bf16[32,16,128]{2,1,0:T(8,128)(2,1)} %get-tuple-element.35), channel_id=1, source_target_pairs={{0,160},{32,192},{64,224},{96,0},{128,32},{160,64},{192,96},{224,1... | collective-permute-start | bytes 393224 | tf_op jit(solution)/shard_map/ppermute | solution.py:299
  119.5 0.7 copy-start.12
  120.1 32.5 %collective-permute-start.3 = (bf16[32,16,128]{2,1,0:T(8,128)(2,1)}, bf16[32,16,128]{2,1,0:T(8,128)(2,1)}, u32[]{:S(2)}, u32[]{:S(2)}) collective-permute-start(bf16[32,16,128]{2,1,0:T(8,128)(2,1)} %get-tuple-element.36), channel_id=1, source_target_pairs={{0,128},{32,160},{64,192},{96,224},{128,0},{160,32},{192,64},{224,... | collective-permute-start | bytes 393224 | tf_op jit(solution)/shard_map/ppermute | solution.py:299
  124.7 0.7 copy-start.14
  125.4 27.3 %collective-permute-start.2 = (bf16[32,16,128]{2,1,0:T(8,128)(2,1)}, bf16[32,16,128]{2,1,0:T(8,128)(2,1)}, u32[]{:S(2)}, u32[]{:S(2)}) collective-permute-start(bf16[32,16,128]{2,1,0:T(8,128)(2,1)} %get-tuple-element.37), channel_id=1, source_target_pairs={{0,96},{32,128},{64,160},{96,192},{128,224},{160,0},{192,32},{224,... | collective-permute-start | bytes 393224 | tf_op jit(solution)/shard_map/ppermute | solution.py:299
  129.2 0.7 copy-start.8
  129.9 22.8 %collective-permute-start.1 = (bf16[32,16,128]{2,1,0:T(8,128)(2,1)}, bf16[32,16,128]{2,1,0:T(8,128)(2,1)}, u32[]{:S(2)}, u32[]{:S(2)}) collective-permute-start(bf16[32,16,128]{2,1,0:T(8,128)(2,1)} %get-tuple-element.38), channel_id=1, source_target_pairs={{0,64},{32,96},{64,128},{96,160},{128,192},{160,224},{192,0},{224,... | collective-permute-start | bytes 393224 | tf_op jit(solution)/shard_map/ppermute | solution.py:299
  136.4 0.6 copy-start.10
  137.0 15.6 %collective-permute-start = (bf16[32,16,128]{2,1,0:T(8,128)(2,1)}, bf16[32,16,128]{2,1,0:T(8,128)(2,1)}, u32[]{:S(2)}, u32[]{:S(2)}) collective-permute-start(bf16[32,16,128]{2,1,0:T(8,128)(2,1)} %get-tuple-element.39), channel_id=1, source_target_pairs={{0,32},{32,64},{64,96},{96,128},{128,160},{160,192},{192,224},{224... | collective-permute-start | bytes 393224 | tf_op jit(solution)/shard_map/ppermute | solution.py:299
  140.2 0.9 copy-start.1
  141.1 0.9 copy-start.3
  142.0 0.9 copy-start.5
  142.9 0.9 copy-start.7
  143.8 0.9 copy-start.13
  144.7 0.9 copy-start.15
  145.6 7.0 %copy-start.9 = (bf16[32,16,128]{2,1,0:T(8,128)(2,1)S(1)}, bf16[32,16,128]{2,1,0:T(8,128)(2,1)}, u32[]{:S(2)}) copy-start(bf16[32,16,128]{2,1,0:T(8,128)(2,1)} %copy-done.8) | copy-start | bytes 393220
  145.6 7.0 %copy-start.11 = (bf16[32,16,128]{2,1,0:T(8,128)(2,1)S(1)}, bf16[32,16,128]{2,1,0:T(8,128)(2,1)}, u32[]{:S(2)}) copy-start(bf16[32,16,128]{2,1,0:T(8,128)(2,1)} %copy-done.10) | copy-start | bytes 393220

commit v5 on v4

--- a/solution.py
+++ b/solution.py
@@ -190,14 +190,18 @@
         far_cos, far_sin = circle(turns(count, lons / 128.0) * (128.0 / lons))
         weight = jnp.where(wave == 0.0, 1.0, 2.0)
         near_cos, near_sin = weight * near_cos, weight * near_sin
-        for b in range(lons // 128):
+        flip = 1.0 - 2.0 * (wave - 2.0 * jnp.floor(wave * 0.5))
+        blocks = lons // 256
+        for b in range(blocks):
             c, s = far_cos[:, b:b + 1], far_sin[:, b:b + 1]
             real = c * near_cos - s * near_sin
             imag = -(s * near_cos + c * near_sin)
-            for row in range(BAND // 8):
-                cut = slice(row * 8, row * 8 + 8)
-                both = jnp.concatenate([real[cut], imag[cut]], axis=0).astype(BF16)
-                out_ref[pl.ds(pl.multiple_of(i * 2 * BAND + row * 16, 16), 16), pl.ds(b * 128, 128)] = both
+            for shift, (first, second) in enumerate(((real, imag), (real * flip, imag * flip))):
+                cols = pl.ds((b + shift * blocks) * 128, 128)
+                for row in range(BAND // 8):
+                    cut = slice(row * 8, row * 8 + 8)
+                    both = jnp.concatenate([first[cut], second[cut]], axis=0).astype(BF16)
+                    out_ref[pl.ds(pl.multiple_of(i * 2 * BAND + row * 16, 16), 16), cols] = both
         return carry
 
     lax.fori_loop(0, wave_ref.shape[0] // BAND, band, 0)

time: 158 us -> 158 us (level)
  no operation moved by 1% of the time
where the time goes in v5:
time: 158 us; the launch traced here: 157 us
  starting transfers between devices  68.9 us (44%)
  Pallas kernels  28.2 us (18%)
  waiting for transfers between devices  24.4 us (15%)
  blocking collectives  22.2 us (14%)
  local copies, waits for them, and re-layouts  12.9 us (8%)
    ppermute x21, starting transfers between devices, hop(): lax.ppermute(blocks[dz], 'z', [(i, (i + dz) % NZ) for i in range(NZ)])  54.9 us
    ppermute x21, waiting for transfers between devices, hop(): lax.ppermute(blocks[dz], 'z', [(i, (i + dz) % NZ) for i in range(NZ)])  24.4 us
    all_to_all x1, blocking collectives, plane(): return lax.all_to_all(block, ('y', 'c', 'mem'), 0, 0, tiled=True)  22.2 us
    all_to_all x2, starting transfers between devices, plane(): return lax.all_to_all(block, ('y', 'c', 'mem'), 0, 0, tiled=True)  14.1 us
    pallas_call x1, Pallas kernels, front(): pl.pallas_call(front_kernel, in_specs=[pl.BlockSpec(memory_space=pltpu.SM...  13.1 us
    pallas_call x2, Pallas kernels, back(): pl.pallas_call(functools.partial(back_kernel, counts=counts), grid=(lons...  11.9 us
    unnamed x36, local copies, waits for them, and re-layouts  11.5 us
  transfers between devices with their start and end apart: 23, of which 8 were waited for; matrix products, arithmetic and copies ran while one was open for 1% of the time, Pallas kernels for 7%

profile of v5, /device:TPU:2, one launch (start us, length us, event | category | flops | bytes accessed | tf_op | source)
XLA Modules:
  0.0 156.9 jit_solution(18040791312566890047)
XLA Ops:
  0.0 13.1 %front.1 = (bf16[32,16,128]{2,1,0:T(8,128)(2,1)}, bf16[32,16,128]{2,1,0:T(8,128)(2,1)}, bf16[32,16,128]{2,1,0:T(8,128)(2,1)}, bf16[32,16,128]{2,1,0:T(8,128)(2,1...) custom-call(s32[1]{0:T(128)} %bitcast.z_ref, ...), custom_call_target="tpu_custom_call" | custom-call | tf_op jit(solution)/shard_map/front/pallas_call | solution.py:142
  13.1 22.2 %all_to_all.15 = bf16[32,8,16,128]{3,2,1,0:T(8,128)(2,1)S(1)} all-to-all(bf16[32,8,16,128]{3,2,1,0:T(8,128)(2,1)} %get-tuple-element.15), channel_id=1, replica_groups=mesh['z'=8,'y'=4,'c'=2,'mem'=4] {'y','c','mem'}, dimensions={0} | all-to-all | bytes 2097152 | tf_op jit(solution)/shard_map/all_to_all | solution.py:312
  35.3 6.6 %all-to-all-start.2 = ((bf16[32,8,16,128]{3,2,1,0:T(8,128)(2,1)}), bf16[32,8,16,128]{3,2,1,0:T(8,128)(2,1)S(1)}, u32[]{:S(2)}, u32[]{:S(2)}) async-start(bf16[32,8,16,128]{3,2,1,0:T(8,128)(2,1)} %get-tuple-element.24), calls=%async_computation.2 | async-start | bytes 2097152 | tf_op jit(solution)/shard_map/all_to_all | solution.py:312
  42.0 2.0 %collective-permute-start.7 = (bf16[32,16,128]{2,1,0:T(8,128)(2,1)}, bf16[32,16,128]{2,1,0:T(8,128)(2,1)S(1)}, u32[]{:S(2)}, u32[]{:S(2)}) collective-permute-start(bf16[32,16,128]{2,1,0:T(8,128)(2,1)} %get-tuple-element.17), channel_id=1, source_target_pairs={{0,32},{32,64},{64,96},{96,128},{128,160},{160,192},{192,224},{224... | collective-permute-start | bytes 393224 | tf_op jit(solution)/shard_map/ppermute | solution.py:303
  44.0 3.3 %collective-permute-start.8 = (bf16[32,16,128]{2,1,0:T(8,128)(2,1)}, bf16[32,16,128]{2,1,0:T(8,128)(2,1)S(1)}, u32[]{:S(2)}, u32[]{:S(2)}) collective-permute-start(bf16[32,16,128]{2,1,0:T(8,128)(2,1)} %get-tuple-element.18), channel_id=1, source_target_pairs={{0,64},{32,96},{64,128},{96,160},{128,192},{160,224},{192,0},{224,... | collective-permute-start | bytes 393224 | tf_op jit(solution)/shard_map/ppermute | solution.py:303
  47.2 4.0 %collective-permute-start.9 = (bf16[32,16,128]{2,1,0:T(8,128)(2,1)}, bf16[32,16,128]{2,1,0:T(8,128)(2,1)S(1)}, u32[]{:S(2)}, u32[]{:S(2)}) collective-permute-start(bf16[32,16,128]{2,1,0:T(8,128)(2,1)} %get-tuple-element.19), channel_id=1, source_target_pairs={{0,96},{32,128},{64,160},{96,192},{128,224},{160,0},{192,32},{224,... | collective-permute-start | bytes 393224 | tf_op jit(solution)/shard_map/ppermute | solution.py:303
  51.8 4.9 %collective-permute-start.11 = (bf16[32,16,128]{2,1,0:T(8,128)(2,1)}, bf16[32,16,128]{2,1,0:T(8,128)(2,1)S(1)}, u32[]{:S(2)}, u32[]{:S(2)}) collective-permute-start(bf16[32,16,128]{2,1,0:T(8,128)(2,1)} %get-tuple-element.21), channel_id=1, source_target_pairs={{0,160},{32,192},{64,224},{96,0},{128,32},{160,64},{192,96},{224,1... | collective-permute-start | bytes 393224 | tf_op jit(solution)/shard_map/ppermute | solution.py:303
  56.8 2.7 %collective-permute-start.12 = (bf16[32,16,128]{2,1,0:T(8,128)(2,1)}, bf16[32,16,128]{2,1,0:T(8,128)(2,1)S(1)}, u32[]{:S(2)}, u32[]{:S(2)}) collective-permute-start(bf16[32,16,128]{2,1,0:T(8,128)(2,1)} %get-tuple-element.22), channel_id=1, source_target_pairs={{0,192},{32,224},{64,0},{96,32},{128,64},{160,96},{192,128},{224,1... | collective-permute-start | bytes 393224 | tf_op jit(solution)/shard_map/ppermute | solution.py:303
  59.4 1.1 collective-permute-done.8.refs_2_
  60.5 3.3 %collective-permute-start.13 = (bf16[32,16,128]{2,1,0:T(8,128)(2,1)}, bf16[32,16,128]{2,1,0:T(8,128)(2,1)S(1)}, u32[]{:S(2)}, u32[]{:S(2)}) collective-permute-start(bf16[32,16,128]{2,1,0:T(8,128)(2,1)} %get-tuple-element.23), channel_id=1, source_target_pairs={{0,224},{32,0},{64,32},{96,64},{128,96},{160,128},{192,160},{224,1... | collective-permute-start | bytes 393224 | tf_op jit(solution)/shard_map/ppermute | solution.py:303
  63.9 5.4 %collective-permute-done.9.refs_3_ = bf16[32,16,128]{2,1,0:T(8,128)(2,1)S(1)} collective-permute-done((bf16[32,16,128]{2,1,0:T(8,128)(2,1)}, bf16[32,16,128]{2,1,0:T(8,128)(2,1)S(1)}, u32[]{:S(2)}, u32[]{:S(2)}) %collective-permute-start.9) | collective-permute-done | bytes 131104 | tf_op jit(solution)/shard_map/ppermute | solution.py:303
  69.3 3.3 %collective-permute-done.11.refs_5_ = bf16[32,16,128]{2,1,0:T(8,128)(2,1)S(1)} collective-permute-done((bf16[32,16,128]{2,1,0:T(8,128)(2,1)}, bf16[32,16,128]{2,1,0:T(8,128)(2,1)S(1)}, u32[]{:S(2)}, u32[]{:S(2)}) %collective-permute-start.11) | collective-permute-done | bytes 131104 | tf_op jit(solution)/shard_map/ppermute | solution.py:303
  72.5 3.4 %collective-permute-done.12.refs_6_ = bf16[32,16,128]{2,1,0:T(8,128)(2,1)S(1)} collective-permute-done((bf16[32,16,128]{2,1,0:T(8,128)(2,1)}, bf16[32,16,128]{2,1,0:T(8,128)(2,1)S(1)}, u32[]{:S(2)}, u32[]{:S(2)}) %collective-permute-start.12) | collective-permute-done | bytes 131104 | tf_op jit(solution)/shard_map/ppermute | solution.py:303
  75.9 0.7 collective-permute-done.13.refs_7_
  76.6 0.9 copy-done.16
  77.5 1.1 stack.1
  78.6 7.4 %all-to-all-start.1 = ((bf16[32,8,16,128]{3,2,1,0:T(8,128)(2,1)}), bf16[32,8,16,128]{3,2,1,0:T(8,128)(2,1)}, u32[]{:S(2)}, u32[]{:S(2)}) async-start(bf16[32,8,16,128]{3,2,1,0:T(8,128)(2,1)} %stack.1), calls=%async_computation.1 | async-start | bytes 2097152 | tf_op jit(solution)/shard_map/all_to_all | solution.py:312
  86.2 2.7 %collective-permute-start.20 = (bf16[32,16,128]{2,1,0:T(8,128)(2,1)S(1)}, bf16[32,16,128]{2,1,0:T(8,128)(2,1)S(1)}, u32[]{:S(2)}, u32[]{:S(2)}) collective-permute-start(bf16[32,16,128]{2,1,0:T(8,128)(2,1)S(1)} %get-tuple-element.25), channel_id=1, source_target_pairs={{0,224},{32,0},{64,32},{96,64},{128,96},{160,128},{192,160},{224,1... | collective-permute-start | bytes 393224 | tf_op jit(solution)/shard_map/ppermute | solution.py:303
  89.0 0.9 collective-permute-start.19
  89.9 3.8 %collective-permute-start.18 = (bf16[32,16,128]{2,1,0:T(8,128)(2,1)S(1)}, bf16[32,16,128]{2,1,0:T(8,128)(2,1)S(1)}, u32[]{:S(2)}, u32[]{:S(2)}) collective-permute-start(bf16[32,16,128]{2,1,0:T(8,128)(2,1)S(1)} %get-tuple-element.27), channel_id=1, source_target_pairs={{0,160},{32,192},{64,224},{96,0},{128,32},{160,64},{192,96},{224,1... | collective-permute-start | bytes 393224 | tf_op jit(solution)/shard_map/ppermute | solution.py:303
  93.7 1.2 collective-permute-start.17
  95.0 3.5 %collective-permute-start.16 = (bf16[32,16,128]{2,1,0:T(8,128)(2,1)S(1)}, bf16[32,16,128]{2,1,0:T(8,128)(2,1)S(1)}, u32[]{:S(2)}, u32[]{:S(2)}) collective-permute-start(bf16[32,16,128]{2,1,0:T(8,128)(2,1)S(1)} %get-tuple-element.29), channel_id=1, source_target_pairs={{0,96},{32,128},{64,160},{96,192},{128,224},{160,0},{192,32},{224,... | collective-permute-start | bytes 393224 | tf_op jit(solution)/shard_map/ppermute | solution.py:303
  98.5 0.9 slice_bitcast_fusion.7
  99.4 2.4 %collective-permute-start.15 = (bf16[32,16,128]{2,1,0:T(8,128)(2,1)S(1)}, bf16[32,16,128]{2,1,0:T(8,128)(2,1)S(1)}, u32[]{:S(2)}, u32[]{:S(2)}) collective-permute-start(bf16[32,16,128]{2,1,0:T(8,128)(2,1)S(1)} %get-tuple-element.30), channel_id=1, source_target_pairs={{0,64},{32,96},{64,128},{96,160},{128,192},{160,224},{192,0},{224,... | collective-permute-start | bytes 393224 | tf_op jit(solution)/shard_map/ppermute | solution.py:303
  101.8 3.7 %collective-permute-done.19 = bf16[32,16,128]{2,1,0:T(8,128)(2,1)S(1)} collective-permute-done((bf16[32,16,128]{2,1,0:T(8,128)(2,1)S(1)}, bf16[32,16,128]{2,1,0:T(8,128)(2,1)S(1)}, u32[]{:S(2)}, u32[]{:S(2)}) %collective-permute-start.19) | collective-permute-done | bytes 131104 | tf_op jit(solution)/shard_map/ppermute | solution.py:303
  105.5 0.6 copy-done
  106.5 0.7 copy-done.2
  107.2 6.9 %collective-permute-start.6 = (bf16[32,16,128]{2,1,0:T(8,128)(2,1)S(1)}, bf16[32,16,128]{2,1,0:T(8,128)(2,1)S(1)}, u32[]{:S(2)}, u32[]{:S(2)}) collective-permute-start(bf16[32,16,128]{2,1,0:T(8,128)(2,1)S(1)} %get-tuple-element.33), channel_id=1, source_target_pairs={{0,224},{32,0},{64,32},{96,64},{128,96},{160,128},{192,160},{224,1... | collective-permute-start | bytes 393224 | tf_op jit(solution)/shard_map/ppermute | solution.py:303
  114.0 0.6 copy-done.4
  114.7 1.1 collective-permute-start.5
  115.8 0.6 copy-done.6
  116.5 3.0 %collective-permute-start.4 = (bf16[32,16,128]{2,1,0:T(8,128)(2,1)}, bf16[32,16,128]{2,1,0:T(8,128)(2,1)}, u32[]{:S(2)}, u32[]{:S(2)}) collective-permute-start(bf16[32,16,128]{2,1,0:T(8,128)(2,1)} %get-tuple-element.35), channel_id=1, source_target_pairs={{0,160},{32,192},{64,224},{96,0},{128,32},{160,64},{192,96},{224,1... | collective-permute-start | bytes 393224 | tf_op jit(solution)/shard_map/ppermute | solution.py:303
  119.5 0.6 copy-done.12
  120.1 4.6 %collective-permute-start.3 = (bf16[32,16,128]{2,1,0:T(8,128)(2,1)}, bf16[32,16,128]{2,1,0:T(8,128)(2,1)}, u32[]{:S(2)}, u32[]{:S(2)}) collective-permute-start(bf16[32,16,128]{2,1,0:T(8,128)(2,1)} %get-tuple-element.36), channel_id=1, source_target_pairs={{0,128},{32,160},{64,192},{96,224},{128,0},{160,32},{192,64},{224,... | collective-permute-start | bytes 393224 | tf_op jit(solution)/shard_map/ppermute | solution.py:303
  124.7 0.7 copy-done.14
  125.4 3.8 %collective-permute-start.2 = (bf16[32,16,128]{2,1,0:T(8,128)(2,1)}, bf16[32,16,128]{2,1,0:T(8,128)(2,1)}, u32[]{:S(2)}, u32[]{:S(2)}) collective-permute-start(bf16[32,16,128]{2,1,0:T(8,128)(2,1)} %get-tuple-element.37), channel_id=1, source_target_pairs={{0,96},{32,128},{64,160},{96,192},{128,224},{160,0},{192,32},{224,... | collective-permute-start | bytes 393224 | tf_op jit(solution)/shard_map/ppermute | solution.py:303
  129.2 0.7 copy-done.8
  129.9 6.5 %collective-permute-done.5 = bf16[32,16,128]{2,1,0:T(8,128)(2,1)S(1)} collective-permute-done((bf16[32,16,128]{2,1,0:T(8,128)(2,1)S(1)}, bf16[32,16,128]{2,1,0:T(8,128)(2,1)S(1)}, u32[]{:S(2)}, u32[]{:S(2)}) %collective-permute-start.5) | collective-permute-done | bytes 131104 | tf_op jit(solution)/shard_map/ppermute | solution.py:303
  136.4 0.6 copy-done.10
  137.3 2.2 %basis.1.refs_9_.refs_8_ = bf16[1024,1536]{1,0:T(8,128)(2,1)S(1)} custom-call(f32[512,128]{1,0:T(8,128)S(1)} %broadcast_in_dim.2.wave_ref), custom_call_target="tpu_custom_call" | custom-call | tf_op jit(solution)/shard_map/basis/pallas_call | solution.py:212
  139.5 0.9 copy-done.1
  140.4 0.9 copy-done.3
  141.4 0.9 copy-done.5
  142.3 0.9 copy-done.7
  143.2 0.9 copy-done.13
  144.1 0.9 copy-done.15
  145.0 7.0 %back.2.refs_10_ = bf16[12,8,1536]{2,1,0:T(8,128)(2,1)} custom-call(bf16[8,4,8,16,128]{4,3,2,1,0:T(8,128)(2,1)} %bitcast.18.refs_0_, bf16[8,4,16,128]{3,2,1,0:T(8,128)(2,1)S(1)} %bitcast.48, bf16[8,4,16,128]{3,2,1,0:T(8,128)(2,1)S(1)} %bitcast.58, bf16[8,4,16,128]{3,2,1,0:T(8,128)(2,1)S(1)} %bitcast.57, bf16[8,4,16,128]{3,2,1,0:T(8,128)(2,1)S(1)} %bitcast.54, ...), custom_call_target="tpu_custom_call" | custom-call | tf_op jit(solution)/shard_map/back/pallas_call | solution.py:287
  152.0 4.9 %back.3 = bf16[12,8,1536]{2,1,0:T(8,128)(2,1)} custom-call(bf16[8,4,16,128]{3,2,1,0:T(8,128)(2,1)S(1)} %bitcast.49, bf16[8,4,16,128]{3,2,1,0:T(8,128)(2,1)} %bitcast.5.refs_1_, bf16[8,4,16,128]{3,2,1,0:T(8,128)(2,1)} %bitcast.7.refs_2_, bf16[8,4,16,128]{3,2,1,0:T(8,128)(2,1)} %bitcast.9.refs_3_, ...), custom_call_target="tpu_custom_call", output_to_operand_aliasing={{}: (10, {})} | custom-call | tf_op jit(solution)/shard_map/back/pallas_call | solution.py:287
  (47 shorter events, 1.5 us)
Async XLA Ops:
  35.3 43.3 %all-to-all-start.2 = ((bf16[32,8,16,128]{3,2,1,0:T(8,128)(2,1)}), bf16[32,8,16,128]{3,2,1,0:T(8,128)(2,1)S(1)}, u32[]{:S(2)}, u32[]{:S(2)}) async-start(bf16[32,8,16,128]{3,2,1,0:T(8,128)(2,1)} %get-tuple-element.24), calls=%async_computation.2 | async-start | bytes 2097152 | tf_op jit(solution)/shard_map/all_to_all | solution.py:312
  42.0 95.1 %copy-start.17 = (s32[512]{0:T(512)S(1)}, s32[512]{0:T(512)}, u32[]{:S(2)}) copy-start(s32[512]{0:T(512)} %param.11) | copy-start | bytes 6148
  42.0 14.8 %collective-permute-start.7 = (bf16[32,16,128]{2,1,0:T(8,128)(2,1)}, bf16[32,16,128]{2,1,0:T(8,128)(2,1)S(1)}, u32[]{:S(2)}, u32[]{:S(2)}) collective-permute-start(bf16[32,16,128]{2,1,0:T(8,128)(2,1)} %get-tuple-element.17), channel_id=1, source_target_pairs={{0,32},{32,64},{64,96},{96,128},{128,160},{160,192},{192,224},{224... | collective-permute-start | bytes 393224 | tf_op jit(solution)/shard_map/ppermute | solution.py:303
  44.0 16.6 %collective-permute-start.8 = (bf16[32,16,128]{2,1,0:T(8,128)(2,1)}, bf16[32,16,128]{2,1,0:T(8,128)(2,1)S(1)}, u32[]{:S(2)}, u32[]{:S(2)}) collective-permute-start(bf16[32,16,128]{2,1,0:T(8,128)(2,1)} %get-tuple-element.18), channel_id=1, source_target_pairs={{0,64},{32,96},{64,128},{96,160},{128,192},{160,224},{192,0},{224,... | collective-permute-start | bytes 393224 | tf_op jit(solution)/shard_map/ppermute | solution.py:303
  47.2 22.0 %collective-permute-start.9 = (bf16[32,16,128]{2,1,0:T(8,128)(2,1)}, bf16[32,16,128]{2,1,0:T(8,128)(2,1)S(1)}, u32[]{:S(2)}, u32[]{:S(2)}) collective-permute-start(bf16[32,16,128]{2,1,0:T(8,128)(2,1)} %get-tuple-element.19), channel_id=1, source_target_pairs={{0,96},{32,128},{64,160},{96,192},{128,224},{160,0},{192,32},{224,... | collective-permute-start | bytes 393224 | tf_op jit(solution)/shard_map/ppermute | solution.py:303
  51.3 18.0 %collective-permute-start.10 = (bf16[32,16,128]{2,1,0:T(8,128)(2,1)}, bf16[32,16,128]{2,1,0:T(8,128)(2,1)S(1)}, u32[]{:S(2)}, u32[]{:S(2)}) collective-permute-start(bf16[32,16,128]{2,1,0:T(8,128)(2,1)} %get-tuple-element.20), channel_id=1, source_target_pairs={{0,128},{32,160},{64,192},{96,224},{128,0},{160,32},{192,64},{224,... | collective-permute-start | bytes 393224 | tf_op jit(solution)/shard_map/ppermute | solution.py:303
  51.8 20.7 %collective-permute-start.11 = (bf16[32,16,128]{2,1,0:T(8,128)(2,1)}, bf16[32,16,128]{2,1,0:T(8,128)(2,1)S(1)}, u32[]{:S(2)}, u32[]{:S(2)}) collective-permute-start(bf16[32,16,128]{2,1,0:T(8,128)(2,1)} %get-tuple-element.21), channel_id=1, source_target_pairs={{0,160},{32,192},{64,224},{96,0},{128,32},{160,64},{192,96},{224,1... | collective-permute-start | bytes 393224 | tf_op jit(solution)/shard_map/ppermute | solution.py:303
  56.8 19.1 %collective-permute-start.12 = (bf16[32,16,128]{2,1,0:T(8,128)(2,1)}, bf16[32,16,128]{2,1,0:T(8,128)(2,1)S(1)}, u32[]{:S(2)}, u32[]{:S(2)}) collective-permute-start(bf16[32,16,128]{2,1,0:T(8,128)(2,1)} %get-tuple-element.22), channel_id=1, source_target_pairs={{0,192},{32,224},{64,0},{96,32},{128,64},{160,96},{192,128},{224,1... | collective-permute-start | bytes 393224 | tf_op jit(solution)/shard_map/ppermute | solution.py:303
  60.5 16.0 %collective-permute-start.13 = (bf16[32,16,128]{2,1,0:T(8,128)(2,1)}, bf16[32,16,128]{2,1,0:T(8,128)(2,1)S(1)}, u32[]{:S(2)}, u32[]{:S(2)}) collective-permute-start(bf16[32,16,128]{2,1,0:T(8,128)(2,1)} %get-tuple-element.23), channel_id=1, source_target_pairs={{0,224},{32,0},{64,32},{96,64},{128,96},{160,128},{192,160},{224,1... | collective-permute-start | bytes 393224 | tf_op jit(solution)/shard_map/ppermute | solution.py:303
  76.6 0.9 copy-start.16
  78.6 61.0 %all-to-all-start.1 = ((bf16[32,8,16,128]{3,2,1,0:T(8,128)(2,1)}), bf16[32,8,16,128]{3,2,1,0:T(8,128)(2,1)}, u32[]{:S(2)}, u32[]{:S(2)}) async-start(bf16[32,8,16,128]{3,2,1,0:T(8,128)(2,1)} %stack.1), calls=%async_computation.1 | async-start | bytes 2097152 | tf_op jit(solution)/shard_map/all_to_all | solution.py:312
  86.2 13.2 %collective-permute-start.20 = (bf16[32,16,128]{2,1,0:T(8,128)(2,1)S(1)}, bf16[32,16,128]{2,1,0:T(8,128)(2,1)S(1)}, u32[]{:S(2)}, u32[]{:S(2)}) collective-permute-start(bf16[32,16,128]{2,1,0:T(8,128)(2,1)S(1)} %get-tuple-element.25), channel_id=1, source_target_pairs={{0,224},{32,0},{64,32},{96,64},{128,96},{160,128},{192,160},{224,1... | collective-permute-start | bytes 393224 | tf_op jit(solution)/shard_map/ppermute | solution.py:303
  89.0 16.5 %collective-permute-start.19 = (bf16[32,16,128]{2,1,0:T(8,128)(2,1)S(1)}, bf16[32,16,128]{2,1,0:T(8,128)(2,1)S(1)}, u32[]{:S(2)}, u32[]{:S(2)}) collective-permute-start(bf16[32,16,128]{2,1,0:T(8,128)(2,1)S(1)} %get-tuple-element.26), channel_id=1, source_target_pairs={{0,192},{32,224},{64,0},{96,32},{128,64},{160,96},{192,128},{224,1... | collective-permute-start | bytes 393224 | tf_op jit(solution)/shard_map/ppermute | solution.py:303
  89.9 16.6 %collective-permute-start.18 = (bf16[32,16,128]{2,1,0:T(8,128)(2,1)S(1)}, bf16[32,16,128]{2,1,0:T(8,128)(2,1)S(1)}, u32[]{:S(2)}, u32[]{:S(2)}) collective-permute-start(bf16[32,16,128]{2,1,0:T(8,128)(2,1)S(1)} %get-tuple-element.27), channel_id=1, source_target_pairs={{0,160},{32,192},{64,224},{96,0},{128,32},{160,64},{192,96},{224,1... | collective-permute-start | bytes 393224 | tf_op jit(solution)/shard_map/ppermute | solution.py:303
  93.7 20.3 %collective-permute-start.17 = (bf16[32,16,128]{2,1,0:T(8,128)(2,1)S(1)}, bf16[32,16,128]{2,1,0:T(8,128)(2,1)S(1)}, u32[]{:S(2)}, u32[]{:S(2)}) collective-permute-start(bf16[32,16,128]{2,1,0:T(8,128)(2,1)S(1)} %get-tuple-element.28), channel_id=1, source_target_pairs={{0,128},{32,160},{64,192},{96,224},{128,0},{160,32},{192,64},{224,... | collective-permute-start | bytes 393224 | tf_op jit(solution)/shard_map/ppermute | solution.py:303
  95.0 20.8 %collective-permute-start.16 = (bf16[32,16,128]{2,1,0:T(8,128)(2,1)S(1)}, bf16[32,16,128]{2,1,0:T(8,128)(2,1)S(1)}, u32[]{:S(2)}, u32[]{:S(2)}) collective-permute-start(bf16[32,16,128]{2,1,0:T(8,128)(2,1)S(1)} %get-tuple-element.29), channel_id=1, source_target_pairs={{0,96},{32,128},{64,160},{96,192},{128,224},{160,0},{192,32},{224,... | collective-permute-start | bytes 393224 | tf_op jit(solution)/shard_map/ppermute | solution.py:303
  99.4 20.1 %collective-permute-start.15 = (bf16[32,16,128]{2,1,0:T(8,128)(2,1)S(1)}, bf16[32,16,128]{2,1,0:T(8,128)(2,1)S(1)}, u32[]{:S(2)}, u32[]{:S(2)}) collective-permute-start(bf16[32,16,128]{2,1,0:T(8,128)(2,1)S(1)} %get-tuple-element.30), channel_id=1, source_target_pairs={{0,64},{32,96},{64,128},{96,160},{128,192},{160,224},{192,0},{224,... | collective-permute-start | bytes 393224 | tf_op jit(solution)/shard_map/ppermute | solution.py:303
  105.5 0.6 copy-start
  106.1 18.6 %collective-permute-start.14 = (bf16[32,16,128]{2,1,0:T(8,128)(2,1)S(1)}, bf16[32,16,128]{2,1,0:T(8,128)(2,1)S(1)}, u32[]{:S(2)}, u32[]{:S(2)}) collective-permute-start(bf16[32,16,128]{2,1,0:T(8,128)(2,1)S(1)} %get-tuple-element.31), channel_id=1, source_target_pairs={{0,32},{32,64},{64,96},{96,128},{128,160},{160,192},{192,224},{224... | collective-permute-start | bytes 393224 | tf_op jit(solution)/shard_map/ppermute | solution.py:303
  106.5 0.7 copy-start.2
  107.2 22.0 %collective-permute-start.6 = (bf16[32,16,128]{2,1,0:T(8,128)(2,1)S(1)}, bf16[32,16,128]{2,1,0:T(8,128)(2,1)S(1)}, u32[]{:S(2)}, u32[]{:S(2)}) collective-permute-start(bf16[32,16,128]{2,1,0:T(8,128)(2,1)S(1)} %get-tuple-element.33), channel_id=1, source_target_pairs={{0,224},{32,0},{64,32},{96,64},{128,96},{160,128},{192,160},{224,1... | collective-permute-start | bytes 393224 | tf_op jit(solution)/shard_map/ppermute | solution.py:303
  114.0 0.6 copy-start.4
  114.7 21.7 %collective-permute-start.5 = (bf16[32,16,128]{2,1,0:T(8,128)(2,1)S(1)}, bf16[32,16,128]{2,1,0:T(8,128)(2,1)S(1)}, u32[]{:S(2)}, u32[]{:S(2)}) collective-permute-start(bf16[32,16,128]{2,1,0:T(8,128)(2,1)S(1)} %get-tuple-element.34), channel_id=1, source_target_pairs={{0,192},{32,224},{64,0},{96,32},{128,64},{160,96},{192,128},{224,1... | collective-permute-start | bytes 393224 | tf_op jit(solution)/shard_map/ppermute | solution.py:303
  115.8 0.6 copy-start.6
  116.5 35.5 %collective-permute-start.4 = (bf16[32,16,128]{2,1,0:T(8,128)(2,1)}, bf16[32,16,128]{2,1,0:T(8,128)(2,1)}, u32[]{:S(2)}, u32[]{:S(2)}) collective-permute-start(bf16[32,16,128]{2,1,0:T(8,128)(2,1)} %get-tuple-element.35), channel_id=1, source_target_pairs={{0,160},{32,192},{64,224},{96,0},{128,32},{160,64},{192,96},{224,1... | collective-permute-start | bytes 393224 | tf_op jit(solution)/shard_map/ppermute | solution.py:303
  119.5 0.7 copy-start.12
  120.1 31.8 %collective-permute-start.3 = (bf16[32,16,128]{2,1,0:T(8,128)(2,1)}, bf16[32,16,128]{2,1,0:T(8,128)(2,1)}, u32[]{:S(2)}, u32[]{:S(2)}) collective-permute-start(bf16[32,16,128]{2,1,0:T(8,128)(2,1)} %get-tuple-element.36), channel_id=1, source_target_pairs={{0,128},{32,160},{64,192},{96,224},{128,0},{160,32},{192,64},{224,... | collective-permute-start | bytes 393224 | tf_op jit(solution)/shard_map/ppermute | solution.py:303
  124.7 0.7 copy-start.14
  125.4 26.6 %collective-permute-start.2 = (bf16[32,16,128]{2,1,0:T(8,128)(2,1)}, bf16[32,16,128]{2,1,0:T(8,128)(2,1)}, u32[]{:S(2)}, u32[]{:S(2)}) collective-permute-start(bf16[32,16,128]{2,1,0:T(8,128)(2,1)} %get-tuple-element.37), channel_id=1, source_target_pairs={{0,96},{32,128},{64,160},{96,192},{128,224},{160,0},{192,32},{224,... | collective-permute-start | bytes 393224 | tf_op jit(solution)/shard_map/ppermute | solution.py:303
  129.2 0.7 copy-start.8
  129.9 22.1 %collective-permute-start.1 = (bf16[32,16,128]{2,1,0:T(8,128)(2,1)}, bf16[32,16,128]{2,1,0:T(8,128)(2,1)}, u32[]{:S(2)}, u32[]{:S(2)}) collective-permute-start(bf16[32,16,128]{2,1,0:T(8,128)(2,1)} %get-tuple-element.38), channel_id=1, source_target_pairs={{0,64},{32,96},{64,128},{96,160},{128,192},{160,224},{192,0},{224,... | collective-permute-start | bytes 393224 | tf_op jit(solution)/shard_map/ppermute | solution.py:303
  136.4 0.6 copy-start.10
  137.0 15.0 %collective-permute-start = (bf16[32,16,128]{2,1,0:T(8,128)(2,1)}, bf16[32,16,128]{2,1,0:T(8,128)(2,1)}, u32[]{:S(2)}, u32[]{:S(2)}) collective-permute-start(bf16[32,16,128]{2,1,0:T(8,128)(2,1)} %get-tuple-element.39), channel_id=1, source_target_pairs={{0,32},{32,64},{64,96},{96,128},{128,160},{160,192},{192,224},{224... | collective-permute-start | bytes 393224 | tf_op jit(solution)/shard_map/ppermute | solution.py:303
  139.5 0.9 copy-start.1
  140.4 0.9 copy-start.3
  141.3 0.9 copy-start.5
  142.3 0.9 copy-start.7
  143.2 0.9 copy-start.13
  144.1 0.9 copy-start.15
  145.0 7.0 %copy-start.9 = (bf16[32,16,128]{2,1,0:T(8,128)(2,1)S(1)}, bf16[32,16,128]{2,1,0:T(8,128)(2,1)}, u32[]{:S(2)}) copy-start(bf16[32,16,128]{2,1,0:T(8,128)(2,1)} %copy-done.8) | copy-start | bytes 393220
  145.0 7.0 %copy-start.11 = (bf16[32,16,128]{2,1,0:T(8,128)(2,1)S(1)}, bf16[32,16,128]{2,1,0:T(8,128)(2,1)}, u32[]{:S(2)}) copy-start(bf16[32,16,128]{2,1,0:T(8,128)(2,1)} %copy-done.10) | copy-start | bytes 393220
